TPU v7x, 128 devices: a whole 4x4x4 slice. The times are simulated.
128 devices in a mesh: gx: 16 (over y, x), gy: 8 (over z, core).
Axes of the slice: x: 4, y: 4, z: 4, core: 2. Of those that a mesh axis runs over, the one named last changes fastest.
Arguments:
- probes: bfloat16 [512, 2048, 256], P('gx', 'gy'), may hold values from -6 to 6
- blk_rows: int32 [16384, 128], P(('gx', 'gy')), may hold values from 0 to 8191
- blk_sensor: int32 [16384], P(('gx', 'gy')), may hold values from 0 to 1023, as said below
- blk_count: int32 [128], P(('gx', 'gy')), may hold values from 64 to 128, as said below
- coef: bfloat16 [16384, 128], P(('gx', 'gy')), may hold values from -5 to 5
- owner: int32 [1024], replicated, may hold values from 0 to 127, as said below
- weights: float32 [1024], replicated, may hold values from 0.1 to 1
Outputs:
- sensitivity: float32 [1024], P(('gx', 'gy'))
- new_weights: float32 [1024], replicated
- density: float32 [512, 2048], P('gx', 'gy')
Inputs may be any that keep to these rules, and one draw needn't show every extreme that they name: `owner`: every device owns exactly 8 sensors. `blk_sensor`: among the live slots of one tile, at most 2 belong to sensors of one owner; in every draw some owner receives 2 live blocks from every tile. `blk_count`: some tile has all 128 slots live.
All inputs are finite; a program needn't handle non-finite values.
Results may differ from a plain program's by a relative error of at most 0.0008.
Values may be sent and summed in bfloat16 or wider, within the bound.
A program may use at most 128 MiB of HBM per device.

v0:
```python
import jax
import jax.numpy as jnp
from jax import lax
from jax.sharding import PartitionSpec as P

SPD = 8
CAP = 2


def over_pieces(shard, axis):
    tiles = lax.all_gather(shard, axis)
    return tiles.sum(axis=0)


def local(probes, blk_rows, blk_sensor, blk_count, coef, owner, weights):
    size_gx = lax.axis_size("gx")
    size_gy = lax.axis_size("gy")
    n_dev = size_gx * size_gy
    me_flat = lax.axis_index("gx") * size_gy + lax.axis_index("gy")
    tile_r, tile_c, probe_n = probes.shape
    nblk, foot = blk_rows.shape
    n_sens = owner.shape[0]
    flat = probes.reshape(tile_r * tile_c, probe_n)
    picked = flat[blk_rows.reshape(-1)].reshape(nblk, foot, probe_n)
    slots = jnp.arange(nblk, dtype=jnp.int32)
    alive = slots < blk_count[0]
    dest = owner[blk_sensor]
    earlier = (dest[:, None] == dest[None, :]) & alive[None, :] & (slots[None, :] < slots[:, None])
    rank = jnp.sum(earlier.astype(jnp.int32), axis=1)
    position = jnp.where(alive, dest * CAP + rank, n_dev * CAP)
    send_rows = (
        jnp.zeros((n_dev * CAP, foot, probe_n), jnp.bfloat16).at[position].set(picked, mode="drop")
    )
    send_coef = jnp.zeros((n_dev * CAP, foot), jnp.bfloat16).at[position].set(coef, mode="drop")
    send_ids = jnp.full((n_dev * CAP,), -1, jnp.int32).at[position].set(blk_sensor, mode="drop")
    recv_rows, recv_coef, recv_ids = (
        lax.all_to_all(send_rows, ("gx", "gy"), split_axis=0, concat_axis=0, tiled=True),
        lax.all_to_all(send_coef, ("gx", "gy"), split_axis=0, concat_axis=0, tiled=True),
        lax.all_to_all(send_ids, ("gx", "gy"), split_axis=0, concat_axis=0, tiled=True),
    )
    my_ids = jnp.nonzero(owner == me_flat, size=SPD, fill_value=0)[0].astype(jnp.int32)
    select = (recv_ids[None, :] == my_ids[:, None]).astype(jnp.bfloat16)
    mixer = select[:, :, None] * recv_coef[None, :, :]
    obs = jnp.einsum("ksr,srp->krp", mixer, recv_rows, preferred_element_type=jnp.float32)
    owned = jnp.sum(obs * obs, axis=(1, 2)) / (foot * probe_n)
    spread = jnp.zeros((n_sens,), jnp.float32).at[my_ids].set(owned)
    sens_all = over_pieces(spread, ("gx", "gy"))
    gain = weights * jnp.sqrt(1.0 + sens_all)
    new_weights = n_sens * gain / jnp.sum(gain)
    values_pts = jnp.where(
        alive[:, None], new_weights[blk_sensor][:, None] * jnp.square(coef.astype(jnp.float32)), 0.0
    )
    density = (
        jnp.zeros((tile_r * tile_c,), jnp.float32)
        .at[blk_rows.reshape(-1)]
        .add(values_pts.reshape(-1))
    )
    return (owned, new_weights, density.reshape(tile_r, tile_c))


def solution(mesh):
    in_specs = (
        P("gx", "gy", None),
        P(("gx", "gy"), None),
        P(("gx", "gy")),
        P(("gx", "gy")),
        P(("gx", "gy"), None),
        P(),
        P(),
    )
    out_specs = (P(("gx", "gy")), P(), P("gx", "gy"))
    return jax.shard_map(local, mesh=mesh, in_specs=in_specs, out_specs=out_specs, check_vma=False)
```

profile of v0, /device:TPU:1, one launch (start us, length us, event | category | flops | bytes accessed | tf_op | source)
XLA Modules:
  0.0 503.9 jit_solution(8996993802345438385)
XLA Ops:
  0.6 0.7 compare_select_fusion.4
  2.0 1.6 gather_fusion
  3.6 0.2 convert_reduce_fusion
  3.8 1.1 scatter_custom_fusion.1
  4.9 0.8 all_to_all.16
  5.7 11.5 %all-to-all-start.1 = ((s32[128,2,1]{1,2,0:T(1,128)}), s32[128,2,1]{1,2,0:T(1,128)S(1)}, u32[]{:S(2)}, u32[]{:S(2)}) async-start(s32[128,2,1]{1,2,0:T(1,128)} %bitcast.7), calls=%async_computation.1 | async-start | bytes 131072 | tf_op jit(solution)/shard_map/all_to_all | solution.py:39
  17.1 0.9 compare_select_fusion
  18.1 1.7 scatter_custom_fusion.3
  19.8 6.8 %all-to-all-done.1 = s32[128,2,1]{1,2,0:T(1,128)S(1)} async-done(((s32[128,2,1]{1,2,0:T(1,128)}), s32[128,2,1]{1,2,0:T(1,128)S(1)}, u32[]{:S(2)}, u32[]{:S(2)}) %all-to-all-start.1) | async-done | bytes 1056 | tf_op jit(solution)/shard_map/all_to_all | solution.py:39
  26.6 4.6 all-to-all-start.2
  31.2 63.5 %gather_fusion.1 = bf16[16384,256]{1,0:T(8,128)(2,1)} fusion(bf16[8192,256]{1,0:T(8,128)(2,1)} %bitcast.28, s32[16384]{0:T(1024)S(1)} %broadcast_clamp_fusion), kind=kCustom, calls=%fused_computation.1 | custom fusion | bytes 16842752 | tf_op jit(solution)/shard_map/gather | solution.py:24
  94.7 6.0 %broadcast_in_dim.36 = bf16[256,128,256]{2,1,0:T(8,128)(2,1)} broadcast(bf16[]{:T(256)} %constant.26.clone.1), dimensions={} | broadcast | bytes 16777218 | tf_op jit(solution)/shard_map/broadcast_in_dim | solution.py:32
  100.7 23.2 %scatter_fusion = bf16[256,128,256]{2,1,0:T(8,128)(2,1)} fusion(bf16[256,128,256]{2,1,0:T(8,128)(2,1)} %broadcast_in_dim.36, s32[128]{0:T(128)S(1)} %fusion.24, bf16[128,128,256]{2,1,0:T(8,128)(2,1)} %bitcast.29), kind=kCustom, calls=%fused_computation.3 | custom fusion | bytes 25166336 | tf_op jit(solution)/shard_map/scatter | solution.py:32
  123.9 10.1 %all-to-all-start = ((bf16[256,128,256]{2,1,0:T(8,128)(2,1)}), bf16[256,128,256]{2,1,0:T(8,128)(2,1)}, u32[]{:S(2)}, u32[]{:S(2)}) async-start(bf16[256,128,256]{2,1,0:T(8,128)(2,1)} %scatter_fusion), calls=%async_computation | async-start | bytes 33554432 | tf_op jit(solution)/shard_map/all_to_all | solution.py:37
  134.0 0.6 convert_reduce_fusion.1
  134.6 0.3 reduce-window.12
  135.2 7.8 %scatter_custom_fusion.2 = s32[8]{0:T(128)S(1)} fusion(s32[1024]{0:T(1024)S(1)} %bitcast.35, s32[1024]{0:T(1024)S(1)} %broadcast.233, s32[]{:T(128)} %constant.27.clone.1), kind=kCustom, calls=%fused_computation.59 | custom fusion | flops 1024 | bytes 36 | tf_op jit(solution)/shard_map/scatter-add | solution.py:41
  143.0 0.2 select_n.113
  143.2 0.7 compare_select_fusion.10
  143.8 0.7 fusion.21
  144.5 0.5 broadcast.255
  145.0 0.8 reduce.6
  145.8 0.1 eq.43
  146.2 208.7 %all-to-all-done = bf16[256,128,256]{2,1,0:T(8,128)(2,1)} async-done(((bf16[256,128,256]{2,1,0:T(8,128)(2,1)}), bf16[256,128,256]{2,1,0:T(8,128)(2,1)}, u32[]{:S(2)}, u32[]{:S(2)}) %all-to-all-start) | async-done | bytes 16777248 | tf_op jit(solution)/shard_map/all_to_all | solution.py:37
  354.9 17.0 %fusion.5 = f32[8]{0:T(128)S(1)} fusion(bf16[256,128,256]{2,1,0:T(8,128)(2,1)} %all-to-all-done, bf16[256,128]{0,1:T(8,128)(2,1)S(1)} %copy.16, bf16[8,256]{1,0:T(8,128)(2,1)S(1)} %compare_convert_fusion), kind=kOutput, calls=%fused_computation.12 | convolution fusion | flops 135004160 | bytes 16846880 | tf_op jit(solution)/shard_map/ksr,srp->krp/dot_general | solution.py:44
  371.9 0.6 scatter_custom_fusion.4
  372.6 42.3 %all-gather = f32[131072]{0:T(1024)S(1)} all-gather(f32[1024]{0:T(1024)S(1)} %scatter_custom_fusion.4), channel_id=2, replica_groups=mesh['gx'=16,'gy'=8] {'gx','gy'}, dimensions={0}, use_global_device_ids=true | all-gather | bytes 528384 | tf_op jit(solution)/shard_map/all_gather | solution.py:11
  415.0 0.6 fusion.18
  415.7 0.7 multiply_divide_fusion
  416.3 1.0 gather_fusion.2
  417.4 85.8 %scatter_custom_fusion.5 = f32[8192]{0:T(1024)S(1)} fusion(s32[16384]{0:T(1024)S(1)} %bitcast.31, f32[16384]{0:T(1024)S(1)} %select_bitcast_fusion, f32[]{:T(128)} %constant.75.clone.1), kind=kCustom, calls=%fused_computation.25 | custom fusion | flops 16384 | bytes 32772 | tf_op jit(solution)/shard_map/scatter-add | solution.py:56
  503.3 0.6 reshape.248
  (28 shorter events, 0.8 us)
Async XLA Ops:
  5.7 20.9 %all-to-all-start.1 = ((s32[128,2,1]{1,2,0:T(1,128)}), s32[128,2,1]{1,2,0:T(1,128)S(1)}, u32[]{:S(2)}, u32[]{:S(2)}) async-start(s32[128,2,1]{1,2,0:T(1,128)} %bitcast.7), calls=%async_computation.1 | async-start | bytes 131072 | tf_op jit(solution)/shard_map/all_to_all | solution.py:39
  26.6 97.3 %all-to-all-start.2 = ((bf16[128,2,128]{2,1,0:T(2,128)(2,1)}), bf16[128,2,128]{2,1,0:T(2,128)(2,1)S(1)}, u32[]{:S(2)}, u32[]{:S(2)}) async-start(bf16[128,2,128]{2,1,0:T(2,128)(2,1)} %bitcast.13), calls=%async_computation.2 | async-start | bytes 131072 | tf_op jit(solution)/shard_map/all_to_all | solution.py:38
  123.8 10.1 %copy-start.1 = (s32[1024]{0:T(1024)S(1)}, s32[1024]{0:T(1024)}, u32[]{:S(2)}) copy-start(s32[1024]{0:T(1024)} %param.12) | copy-start | bytes 12292
  123.9 231.1 %all-to-all-start = ((bf16[256,128,256]{2,1,0:T(8,128)(2,1)}), bf16[256,128,256]{2,1,0:T(8,128)(2,1)}, u32[]{:S(2)}, u32[]{:S(2)}) async-start(bf16[256,128,256]{2,1,0:T(8,128)(2,1)} %scatter_fusion), calls=%async_computation | async-start | bytes 33554432 | tf_op jit(solution)/shard_map/all_to_all | solution.py:37
  146.2 268.9 %copy-start.3 = (f32[1024]{0:T(1024)S(1)}, f32[1024]{0:T(1024)}, u32[]{:S(2)}) copy-start(f32[1024]{0:T(1024)} %param.13) | copy-start | bytes 12292
  146.2 271.1 %copy-start.2 = (bf16[128,128]{1,0:T(8,128)(2,1)S(1)}, bf16[128,128]{1,0:T(8,128)(2,1)}, u32[]{:S(2)}) copy-start(bf16[128,128]{1,0:T(8,128)(2,1)} %param.11) | copy-start | bytes 98308
  371.9 132.0 %copy-start.4 = (f32[8]{0:T(128)}, f32[8]{0:T(128)S(1)}, u32[]{:S(2)}) copy-start(f32[8]{0:T(128)S(1)} %broadcast_multiply_fusion) | copy-start | bytes 100
  416.3 87.6 %copy-start = (f32[1024]{0:T(1024)}, f32[1024]{0:T(1024)S(1)}, u32[]{:S(2)}) copy-start(f32[1024]{0:T(1024)S(1)} %multiply_divide_fusion) | copy-start | bytes 12292
where the time goes:
time: 505 us; the launch traced here: 504 us
  waiting for transfers between devices  216 us (43%)
  local copies, waits for them, and re-layouts  101 us (20%)
  other arithmetic  100 us (20%)
  blocking collectives  42.3 us (8%)
  starting transfers between devices  26.2 us (5%)
  matrix products  17 us (3%)
    all_to_all x1, waiting for transfers between devices, local(): lax.all_to_all(send_rows, ('gx', 'gy'), split_axis=0, concat_axis=0, tile...  209 us
    scatter-add x1, other arithmetic, local(): density = jnp.zeros((tile_r * tile_c,), jnp.float32).at[blk_rows.reshape(...  85.8 us
    gather x1, local copies, waits for them, and re-layouts, local(): picked = flat[blk_rows.reshape(-1)].reshape(nblk, foot, probe_n)  63.5 us
    all_gather x1, blocking collectives, over_pieces(): tiles = lax.all_gather(shard, axis)  42.3 us
    scatter x1, local copies, waits for them, and re-layouts, local(): jnp.zeros((n_dev * CAP, foot, probe_n), jnp.bfloat16).at[position]  23.2 us
    dot_general x1, matrix products, local(): jnp.einsum('ksr,srp->krp', mixer, recv_rows, preferred_element_type=jnp.f...  17 us
    all_to_all x1, starting transfers between devices, local(): lax.all_to_all(send_ids, ('gx', 'gy'), split_axis=0, concat_axis=0, tiled...  11.5 us
  transfers between devices with their start and end apart: 3, of which 2 were waited for; matrix products, arithmetic and copies ran while one was open for 21% of the time, Pallas kernels for 0%

commit v1 on v0

v1 whole, which is shorter than its diff:
```python
import functools

import jax
import jax.numpy as jnp
from jax import lax
from jax.experimental import pallas as pl
from jax.experimental.pallas import tpu as pltpu
from jax.sharding import PartitionSpec as P

MESH = pl.DeviceIdType.MESH
HIGHEST = lax.Precision.HIGHEST
STRIDE = 37
GROUP = 4
MROWS = 256


def shifted(step):
    off = lax.rem((step + 1) * STRIDE, 128)
    gx, gy = lax.axis_index("gx"), lax.axis_index("gy")
    y = lax.rem(gx // 4 + off // 32, 4)
    x = lax.rem(lax.rem(gx, 4) + lax.rem(off // 8, 4), 4)
    z = lax.rem(gy // 2 + lax.rem(off // 2, 4), 4)
    core = lax.rem(lax.rem(gy, 2) + lax.rem(off, 2), 2)
    return y * 4 + x, z * 2 + core


def kernel(
    rows_s, probes, meta, rows_v, coef_v, ids_v, owner_v, weights_v,
    sens_o, new_o, dens_o,
    tile, stage, send, recv, meta_in, dens, obs, h_send, h_in, h_mid, h_in2, wide,
    data_ss, data_rs, meta_ss, meta_rs, h_ss, h_rs, h2_ss, h2_rs,
):
    n_pts, probe_n = probes.shape
    foot = 128
    gx, gy = lax.axis_index("gx"), lax.axis_index("gy")
    me = gx * 8 + gy

    barrier = pltpu.get_barrier_semaphore()

    def greet(step, c):
        pl.semaphore_signal(barrier, inc=1, device_id=shifted(step), device_id_type=MESH)
        return c

    lax.fori_loop(0, 127, greet, 0)

    def widen(i, c):
        part = pl.ds(pl.multiple_of(i * 64, 64), 64)
        block = probes[part, :].astype(jnp.float32)
        tile[part, 0, :] = block[:, :128]
        tile[part, 1, :] = block[:, 128:]
        return c

    lax.fori_loop(0, n_pts // 64, widen, 0)
    pl.semaphore_wait(barrier, 127)

    def data_copy(step):
        return pltpu.make_async_remote_copy(
            src_ref=send.at[step], dst_ref=recv.at[step],
            send_sem=data_ss.at[step], recv_sem=data_rs.at[step],
            device_id=shifted(step), device_id_type=MESH,
        )

    def meta_copy(step):
        tx, ty = shifted(step)
        return pltpu.make_async_remote_copy(
            src_ref=meta.at[tx * 8 + ty], dst_ref=meta_in.at[step],
            send_sem=meta_ss.at[step], recv_sem=meta_rs.at[step],
            device_id=(tx, ty), device_id_type=MESH,
        )

    def gather(step, c):
        tx, ty = shifted(step)
        base = (tx * 8 + ty) * 128
        for i in range(128):
            stage[i] = tile[rows_s[base + i]]

        @pl.when(step >= 1)
        def _():
            meta_copy(step - 1).start()
            data_copy(step - 1).start()

        send[step, :, :128] = stage[:, 0, :].astype(jnp.bfloat16)
        send[step, :, 128:] = stage[:, 1, :].astype(jnp.bfloat16)
        return c

    lax.fori_loop(0, 128, gather, 0)
    recv[127] = send[127]
    meta_in[127] = meta[me]

    q = lax.broadcasted_iota(jnp.int32, (64, 128), 0)
    hi_of = jnp.where(q < 32, 2 * q, 2 * q - 63)
    lo_of = lax.broadcasted_iota(jnp.int32, (128, 128), 0)

    def spread(slot, c):
        row = rows_v[pl.ds(slot, 1), :]
        val = coef_v[pl.ds(slot, 1), :]
        high = jnp.where(row // 128 == hi_of, val, 0.0).astype(jnp.bfloat16)
        low = jnp.where(lax.rem(row, 128) == lo_of, val, 0.0).astype(jnp.bfloat16)
        dens[slot] = lax.dot_general(
            high, low, (((1,), (1,)), ((), ())), preferred_element_type=jnp.float32
        )
        return c

    lax.fori_loop(0, 128, spread, 0)

    obs[...] = jnp.zeros_like(obs)
    sens_of = lax.broadcasted_iota(jnp.int32, (MROWS, 128), 0).astype(jnp.float32)

    def mix(g, c):
        for k in range(GROUP):
            step = g * GROUP + k

            @pl.when(step < 127)
            def _():
                meta_copy(step).wait_recv()
                data_copy(step).wait_recv()

        cols = jnp.concatenate([recv[g * GROUP + k] for k in range(GROUP)], axis=0)
        for m in range(1024 // MROWS):
            mixer = jnp.concatenate(
                [
                    jnp.where(
                        meta_in[g * GROUP + k, 1:2, :] - float(m * MROWS) == sens_of,
                        meta_in[g * GROUP + k, 0:1, :], 0.0,
                    ).astype(jnp.bfloat16)
                    for k in range(GROUP)
                ],
                axis=1,
            )
            obs[m * MROWS:(m + 1) * MROWS, :] += jnp.dot(
                mixer, cols, preferred_element_type=jnp.float32
            )
        return c

    lax.fori_loop(0, 128 // GROUP, mix, 0)

    ones = jnp.ones((8, 128), jnp.float32)
    for k in range(8):
        part = obs[k * 128:(k + 1) * 128, :]
        part = part * part
        part = part[:, :128] + part[:, 128:]
        h_send[k:k + 1, :] = lax.dot_general(
            ones, part, (((1,), (1,)), ((), ())),
            preferred_element_type=jnp.float32, precision=HIGHEST,
        )[0:1, :] * (1.0 / (foot * probe_n))

    def first_copy(k):
        to = lax.rem(gy + k, 8)
        return pltpu.make_async_remote_copy(
            src_ref=h_send, dst_ref=h_in.at[gy],
            send_sem=h_ss.at[k], recv_sem=h_rs.at[k],
            device_id=(gx, to), device_id_type=MESH,
        )

    def second_copy(k):
        to = lax.rem(gx + k, 16)
        return pltpu.make_async_remote_copy(
            src_ref=h_mid, dst_ref=h_in2.at[gx],
            send_sem=h2_ss.at[k], recv_sem=h2_rs.at[k],
            device_id=(to, gy), device_id_type=MESH,
        )

    for k in range(1, 8):
        first_copy(k).start()
    h_in[gy] = h_send[...]
    mine = owner_v[...] == me
    count = jnp.where(mine, 1.0, 0.0)
    before = jnp.where(
        lax.broadcasted_iota(jnp.int32, (128, 128), 0) < lax.broadcasted_iota(jnp.int32, (128, 128), 1),
        1.0, 0.0,
    )
    above = jnp.where(
        lax.broadcasted_iota(jnp.int32, (8, 8), 1) < lax.broadcasted_iota(jnp.int32, (8, 8), 0),
        1.0, 0.0,
    )
    in_row = jnp.dot(count, before, precision=HIGHEST, preferred_element_type=jnp.float32)
    rank = in_row + jnp.dot(
        above, jnp.broadcast_to(jnp.sum(count, axis=1, keepdims=True), (8, 128)),
        precision=HIGHEST, preferred_element_type=jnp.float32,
    )
    rank = jnp.where(mine, rank, -1.0)
    for k in range(1, 8):
        first_copy(k).wait_recv()
    total = h_in[0]
    for k in range(1, 8):
        total = total + h_in[k]
    h_mid[...] = total
    for k in range(1, 16):
        second_copy(k).start()
    h_in2[gx] = total
    for k in range(1, 16):
        second_copy(k).wait_recv()
    total = h_in2[0]
    for k in range(1, 16):
        total = total + h_in2[k]

    gain = weights_v[...] * jnp.sqrt(1.0 + total)
    new = 1024.0 * gain / jnp.sum(gain)
    new_o[...] = new
    for k in range(8):
        sens_o[k:k + 1, :] = jnp.broadcast_to(
            jnp.sum(jnp.where(rank == float(k), total, 0.0), keepdims=True), (1, 128)
        )

    ids = ids_v[...]
    lane = lax.broadcasted_iota(jnp.int32, (128, 128), 1)
    picked = jnp.zeros((128, 128), jnp.float32)
    for k in range(8):
        picked = picked + jnp.where(ids == lane + k * 128, new_o[k:k + 1, :], 0.0)
    wide[...] = jnp.broadcast_to(jnp.sum(picked, axis=1, keepdims=True), (128, 128))

    def weigh(i, acc):
        for u in range(8):
            slot = i * 8 + u
            acc = acc + wide[pl.ds(slot, 1), :] * dens[slot]
        return acc

    out = lax.fori_loop(0, 16, weigh, jnp.zeros((64, 128), jnp.float32))
    dens_o[:, :128] = out[:32]
    dens_o[:, 128:] = out[32:]

    def drain(step, c):
        meta_copy(step).wait_send()
        data_copy(step).wait_send()
        return c

    lax.fori_loop(0, 127, drain, 0)
    for k in range(1, 8):
        first_copy(k).wait_send()
    for k in range(1, 16):
        second_copy(k).wait_send()


def local(probes, blk_rows, blk_sensor, blk_count, coef, owner, weights):
    tile_r, tile_c, probe_n = probes.shape
    nblk, foot = blk_rows.shape
    alive = jnp.arange(nblk, dtype=jnp.int32) < blk_count[0]
    coef_m = jnp.where(alive[:, None], coef.astype(jnp.float32), 0.0)
    rows_t = blk_rows.T.reshape(-1)
    ids = jnp.broadcast_to(blk_sensor.astype(jnp.float32)[None, :], (foot, nblk))
    meta = jnp.stack([coef_m.T, ids], axis=1)
    ids_v = jnp.broadcast_to(blk_sensor[:, None], (nblk, 128))
    vmem = pl.BlockSpec(memory_space=pltpu.VMEM)
    smem = pl.BlockSpec(memory_space=pltpu.SMEM)
    f32 = jnp.float32
    sens, new, dens = pl.pallas_call(
        kernel,
        out_shape=(
            jax.ShapeDtypeStruct((8, 128), f32),
            jax.ShapeDtypeStruct((8, 128), f32),
            jax.ShapeDtypeStruct((tile_r, tile_c), f32),
        ),
        in_specs=[smem] + [vmem] * 7,
        out_specs=(vmem, vmem, vmem),
        scratch_shapes=[
            pltpu.VMEM((tile_r * tile_c, 2, 128), f32),
            pltpu.VMEM((nblk, 2, 128), f32),
            pltpu.VMEM((128, nblk, probe_n), jnp.bfloat16),
            pltpu.VMEM((128, nblk, probe_n), jnp.bfloat16),
            pltpu.VMEM((128, 2, 128), f32),
            pltpu.VMEM((nblk, 64, 128), f32),
            pltpu.VMEM((1024, probe_n), f32),
            pltpu.VMEM((8, 128), f32),
            pltpu.VMEM((8, 8, 128), f32),
            pltpu.VMEM((8, 128), f32),
            pltpu.VMEM((16, 8, 128), f32),
            pltpu.VMEM((128, 128), f32),
            pltpu.SemaphoreType.DMA((128,)),
            pltpu.SemaphoreType.DMA((128,)),
            pltpu.SemaphoreType.DMA((128,)),
            pltpu.SemaphoreType.DMA((128,)),
            pltpu.SemaphoreType.DMA((8,)),
            pltpu.SemaphoreType.DMA((8,)),
            pltpu.SemaphoreType.DMA((16,)),
            pltpu.SemaphoreType.DMA((16,)),
        ],
        compiler_params=pltpu.CompilerParams(
            collective_id=0, has_side_effects=True, vmem_limit_bytes=60 * 2 ** 20
        ),
        name="exchange",
    )(
        rows_t, probes.reshape(tile_r * tile_c, probe_n), meta, blk_rows, coef_m, ids_v,
        owner.reshape(8, 128), weights.reshape(8, 128),
    )
    return sens[:, 0], new.reshape(-1), dens


def solution(mesh):
    in_specs = (
        P("gx", "gy", None),
        P(("gx", "gy"), None),
        P(("gx", "gy")),
        P(("gx", "gy")),
        P(("gx", "gy"), None),
        P(),
        P(),
    )
    out_specs = (P(("gx", "gy")), P(), P("gx", "gy"))
    return jax.shard_map(local, mesh=mesh, in_specs=in_specs, out_specs=out_specs, check_vma=False)
```

time: 505 us -> 160 us (0.32)
  waiting for transfers between devices: 216 us -> 0 us
  Pallas kernels: 0 us -> 149 us
  other arithmetic: 100 us -> 2.14 us
  local copies, waits for them, and re-layouts: 101 us -> 7.67 us
  blocking collectives: 42.3 us -> 0 us
  starting transfers between devices: 26.2 us -> 0 us
  matrix products: 17 us -> 0 us
    all_to_all x3 -> x0, waiting for transfers between devices: 216 us -> none  [the longest x1 209 us: local(): lax.all_to_all(send_rows, ('gx', 'gy'), split_axis=0, concat_axis=0, tile...]
    pallas_call x0 -> x1, Pallas kernels: none -> 149 us  [local(): pl.pallas_call(kernel, out_shape=(jax.ShapeDtypeStruct((8, 128), f32), ja...]
    scatter-add x2 -> x0, other arithmetic: 93.6 us -> none  [the longest x1 85.8 us: local(): density = jnp.zeros((tile_r * tile_c,), jnp.float32).at[blk_rows.reshape(...]
    gather x3 -> x0, local copies, waits for them, and re-layouts: 66.1 us -> none  [the longest x1 63.5 us: local(): picked = flat[blk_rows.reshape(-1)].reshape(nblk, foot, probe_n)]
    all_gather x1 -> x0, blocking collectives: 42.3 us -> none  [over_pieces(): tiles = lax.all_gather(shard, axis)]
    scatter x4 -> x0, local copies, waits for them, and re-layouts: 26.6 us -> none  [the longest x1 23.2 us: local(): jnp.zeros((n_dev * CAP, foot, probe_n), jnp.bfloat16).at[position]]
    all_to_all x3 -> x0, starting transfers between devices: 26.2 us -> none  [the longest x1 11.5 us: local(): lax.all_to_all(send_ids, ('gx', 'gy'), split_axis=0, concat_axis=0, tiled...]
    dot_general x1 -> x0, matrix products: 17 us -> none  [local(): jnp.einsum('ksr,srp->krp', mixer, recv_rows, preferred_element_type=jnp.f...]
  transfers between devices with their start and end apart: 3 -> 0, of which waited for: 2 -> 0; matrix products, arithmetic and copies ran while one was open for 21% -> 0% of each run, Pallas kernels for 0% -> 0%
where the time goes in v1:
time: 160 us
  Pallas kernels  149 us (93%)
  local copies, waits for them, and re-layouts  7.67 us (5%)
  other arithmetic  2.14 us (1%)
    pallas_call x1, Pallas kernels, local(): pl.pallas_call(kernel, out_shape=(jax.ShapeDtypeStruct((8, 128), f32), ja...  149 us
    unnamed x3, local copies, waits for them, and re-layouts  4.2 us

profile of v1, /device:TPU:1, one launch (start us, length us, event | category | flops | bytes accessed | tf_op | source)
XLA Modules:
  0.0 159.6 jit_solution(2469190665369090995)
XLA Ops:
  1.3 1.5 convert_select_fusion
  2.8 0.7 convert_element_type.7
  3.4 0.1 stack_broadcast_in_dim.2
  3.5 0.7 copy.12.meta
  4.2 1.6 copy.11
  5.8 1.4 broadcast_in_dim.22.ids_v
  7.2 148.5 %exchange.1 = (f32[8,128]{1,0:T(8,128)}, f32[8,128]{1,0:T(8,128)}, f32[32,256]{1,0:T(8,128)}) custom-call(s32[16384]{0:T(1024)} %bitcast.14, bf16[8192,256]{1,0:T(8,128)(2,1)} %bitcast.13, f32[128,2,128]{2,1,0:T(2,128)} %copy.12.meta, s32[128,128]{1,0:T(8,128)} %rows_v.1, f32[128,128]{1,0:T(8,128)} %get-tuple-element.9.coef_v, ...), custom_call_target="tpu_custom_call" | custom-call | tf_op jit(solution)/shard_map/exchange/pallas_call | solution.py:246
  155.7 1.3 slice_reduce_fusion
  157.0 1.3 copy.16
  158.2 1.4 copy.17
  (2 shorter events, 0.0 us)

commit v2 on v1

v2 whole, which is shorter than its diff:
```python
import jax
import jax.numpy as jnp
from jax import lax
from jax.experimental import pallas as pl
from jax.experimental.pallas import tpu as pltpu
from jax.sharding import PartitionSpec as P

MESH = pl.DeviceIdType.MESH
HIGHEST = lax.Precision.HIGHEST
FIRST = (0, 1, 2, 2)
SECOND = (1, 2, 0, 0)
THIRD = (2, 0, 1, 1)


def place():
    gx, gy = lax.axis_index("gx"), lax.axis_index("gy")
    return [lax.rem(gx, 4), gx // 4, gy // 2], lax.rem(gy, 2)


def peer(axis, off, core_off):
    at, core = place()
    at[axis] = lax.rem(at[axis] + off, 4)
    return at[1] * 4 + at[0], at[2] * 2 + lax.rem(core + core_off, 2)


def order(i):
    return lax.rem(1 + 2 * i - 3 * (i // 2), 4)


def decode(pos):
    return order(pos // 8), order(lax.rem(pos, 4)), lax.rem(pos, 8) // 4


def kernel(
    rows_s, probes, meta, rows_v, coef_v, ids_v, owner_v, weights_v,
    sens_o, new_o, dens_o,
    tile, stage, send, zone, metas, dens, part, final, steps_v, h_send, h_in, h_mid, h_in2, wide,
    ss1, rs1, ss2, rs2, ms1, mr1, ms2, mr2, fs, fr, h_ss, h_rs, h2_ss, h2_rs,
):
    n_pts, probe_n = probes.shape
    foot = 128
    gx, gy = lax.axis_index("gx"), lax.axis_index("gy")
    me = gx * 8 + gy
    at, core = place()
    bf16, f32 = jnp.bfloat16, jnp.float32

    barrier = pltpu.get_barrier_semaphore()

    def greet(device):
        pl.semaphore_signal(barrier, inc=1, device_id=device, device_id_type=MESH)

    for k in range(1, 16):
        greet((lax.rem(gx // 4 + k // 4, 4) * 4 + lax.rem(lax.rem(gx, 4) + k % 4, 4), gy))
    for k in range(1, 8):
        greet((gx, lax.rem(gy + k, 8)))
    for axis in (0, 1):
        for off in (1, 2, 3):
            greet(peer(axis, off, 1))

    flat = tile.reshape(2 * n_pts, 128)

    def widen(i, c):
        block = probes[pl.ds(pl.multiple_of(i * 64, 64), 64), :].astype(f32)
        flat[pl.ds(i * 128, 64, 2), :] = block[:, :128]
        flat[pl.ds(i * 128 + 1, 64, 2), :] = block[:, 128:]
        return c

    lax.fori_loop(0, n_pts // 64, widen, 0)
    for i in range(16):
        steps_v[i * 16:(i + 1) * 16, :] = (
            lax.broadcasted_iota(jnp.int32, (16, 128), 0) + i * 16
        ).astype(f32).astype(bf16)
    pl.semaphore_wait(barrier, 28)

    def meta1(k, of, oc):
        first = lax.rem(core + oc, 2) * 64 + k * 16 + lax.rem(at[FIRST[k]] + of, 4) * 4
        src = oc * 4 + of
        return pltpu.make_async_remote_copy(
            src_ref=meta.at[pl.ds(first, 4)], dst_ref=metas.at[k, pl.ds(0, 4), src],
            send_sem=ms1.at[k, src], recv_sem=mr1.at[k, src],
            device_id=peer(FIRST[k], of, oc), device_id_type=MESH,
        )

    def meta2(k, og):
        return pltpu.make_async_remote_copy(
            src_ref=metas.at[k, lax.rem(at[SECOND[k]] + og, 4)], dst_ref=metas.at[k, 4 + og],
            send_sem=ms2.at[k, og], recv_sem=mr2.at[k, og],
            device_id=peer(SECOND[k], og, 0), device_id_type=MESH,
        )

    def copy1(k, pos):
        og, of, oc = decode(pos)
        return pltpu.make_async_remote_copy(
            src_ref=send.at[k, pos], dst_ref=zone.at[k, og + 3 * ((og + 3) // 4), oc * 4 + of],
            send_sem=ss1.at[k, pos], recv_sem=rs1.at[k, pos],
            device_id=peer(FIRST[k], of, oc), device_id_type=MESH,
        )

    def copy2(k, pos):
        og, of, oc = decode(pos)
        return pltpu.make_async_remote_copy(
            src_ref=zone.at[k, 3 + og, oc * 4 + of], dst_ref=zone.at[k, og, oc * 4 + of],
            send_sem=ss2.at[k, pos], recv_sem=rs2.at[k, pos],
            device_id=peer(SECOND[k], og, 0), device_id_type=MESH,
        )

    def copy3(k, oh):
        block = lax.rem(at[THIRD[k]] + oh, 4)
        return pltpu.make_async_remote_copy(
            src_ref=part.at[k, pl.ds(pl.multiple_of(block * 256, 256), 256)], dst_ref=final.at[k, oh - 1],
            send_sem=fs.at[k, oh], recv_sem=fr.at[k, oh],
            device_id=peer(THIRD[k], oh, 0), device_id_type=MESH,
        )

    others = [(of, oc) for oc in (0, 1) for of in (1, 3, 2, 0) if (of, oc) != (0, 0)]
    for of, oc in others:
        for k in range(4):
            meta1(k, of, oc).start()
    for k in range(4):
        metas[k, 0:4, 0] = meta[pl.ds(core * 64 + k * 16 + at[FIRST[k]] * 4, 4)]

    def gather(k, pos, buf):
        og, of, oc = decode(pos)
        chan = (
            lax.rem(core + oc, 2) * 64 + k * 16
            + lax.rem(at[FIRST[k]] + of, 4) * 4 + lax.rem(at[SECOND[k]] + og, 4)
        )
        base = chan * 128
        for i in range(128):
            stage[buf, 2 * i:2 * i + 2, :] = tile[rows_s[base + i]]
        send[k, pos, :, :128] = stage[buf, pl.ds(0, 128, 2), :].astype(bf16)
        send[k, pos, :, 128:] = stage[buf, pl.ds(1, 128, 2), :].astype(bf16)

    def give(k, pos):
        mine = lax.rem(pos, 8) == 3

        @pl.when(mine)
        def _():
            og, _, _ = decode(pos)
            zone[k, og + 3 * ((og + 3) // 4), 0] = send[k, pos]

        @pl.when(jnp.logical_not(mine))
        def _():
            copy1(k, pos).start()

    def first_loop(pos, c):
        gather(0, pos, 0)

        @pl.when(pos > 0)
        def _():
            give(2, pos - 1)

        gather(1, pos, 1)
        give(0, pos)
        gather(2, pos, 2)
        give(1, pos)
        return c

    lax.fori_loop(0, 32, first_loop, 0)

    def second_loop(pos, c):
        gather(3, pos, 0)

        @pl.when(pos == 0)
        def _():
            give(2, 31)

        @pl.when(pos > 0)
        def _():
            give(3, pos - 1)
        return c

    lax.fori_loop(0, 32, second_loop, 0)
    give(3, 31)

    for of, oc in others:
        for k in range(4):
            meta1(k, of, oc).wait_recv()
    for og in (1, 3, 2):
        for k in range(4):
            meta2(k, og).start()

    q = lax.broadcasted_iota(jnp.int32, (64, 128), 0)
    hi_of = jnp.where(q < 32, 2 * q, 2 * q - 63)
    lo_of = lax.broadcasted_iota(jnp.int32, (128, 128), 0)

    def spread(first):
        for u in range(4):
            row = rows_v[pl.ds(first + u, 1), :]
            val = coef_v[pl.ds(first + u, 1), :]
            high = jnp.where(row // 128 == hi_of, val, 0.0).astype(bf16)
            low = jnp.where(lax.rem(row, 128) == lo_of, val, 0.0).astype(bf16)
            dens[first + u] = lax.dot_general(
                high, low, (((1,), (1,)), ((), ())), preferred_element_type=f32
            )

    def forward(k, pos):
        @pl.when(lax.rem(pos, 8) != 3)
        def _():
            copy1(k, pos).wait_recv()

        copy2(k, pos).start()

    def forward_loop(pos, c):
        spread(pos * 4)
        for k in range(3):
            forward(k, pos)
        return c

    lax.fori_loop(0, 24, forward_loop, 0)
    part[...] = jnp.zeros_like(part)

    def mix(k, group):
        pos = group * 4
        og, _, oc = decode(pos)
        for u in range(4):
            @pl.when(pos + u < 24)
            def _():
                copy2(k, pos + u).wait_recv()

            @pl.when(jnp.logical_and(pos + u >= 24, pos + u != 27))
            def _():
                copy1(k, pos + u).wait_recv()

        cols = zone[k, og, pl.ds(oc * 4, 4)].reshape(512, probe_n)
        slot = og + 4 * ((og + 3) // 4) + at[SECOND[k]] * (1 - (og + 3) // 4)
        tags = [metas[k, slot, oc * 4 + u] for u in range(4)]
        vals = [jnp.broadcast_to(t[0:1], (16, 128)).astype(bf16) for t in tags]
        zero = jnp.zeros((16, 128), bf16)
        for m in range(4):
            names = [jnp.broadcast_to(t[1:2] - float(m * 256), (16, 128)).astype(bf16) for t in tags]
            mixer = jnp.concatenate(
                [
                    jnp.concatenate(
                        [
                            jnp.where(names[u] == steps_v[i * 16:(i + 1) * 16, :], vals[u], zero)
                            for i in range(16)
                        ],
                        axis=0,
                    )
                    for u in range(4)
                ],
                axis=1,
            )
            part[k, m * 256:(m + 1) * 256, :] += jnp.dot(mixer, cols, preferred_element_type=f32)

    def late_loop(i, c):
        @pl.when(i == 0)
        def _():
            for og in (1, 3, 2):
                for k in range(4):
                    meta2(k, og).wait_recv()

        spread(96 + i * 4)
        for u in range(3):
            forward(3, i * 3 + u)
        mix(0, lax.rem(i + 6, 8))
        return c

    lax.fori_loop(0, 8, late_loop, 0)
    for oh in (1, 3, 2):
        copy3(0, oh).start()

    def mix_loop(k):
        def body(i, c):
            mix(k, lax.rem(i + 6, 8))
            return c

        lax.fori_loop(0, 8, body, 0)
        for oh in (1, 3, 2):
            copy3(k, oh).start()

    mix_loop(2)
    mix_loop(1)
    mix_loop(3)

    h_send[...] = jnp.zeros_like(h_send)
    ones = jnp.ones((8, 128), f32)
    for k in (0, 2, 1, 3):
        for oh in (1, 3, 2):
            copy3(k, oh).wait_recv()
        block = at[THIRD[k]]
        whole = part[k, pl.ds(pl.multiple_of(block * 256, 256), 256), :]
        for i in range(3):
            whole = whole + final[k, i]
        whole = whole * whole
        sums = lax.dot_general(
            ones, whole[:, :128] + whole[:, 128:], (((1,), (1,)), ((), ())),
            preferred_element_type=f32, precision=HIGHEST,
        ) * (1.0 / (foot * probe_n))
        for i in range(2):
            h_send[pl.ds(2 * block + i, 1), :] += sums[0:1, i * 128:(i + 1) * 128]

    def first_copy(k):
        to = lax.rem(gy + k, 8)
        return pltpu.make_async_remote_copy(
            src_ref=h_send, dst_ref=h_in.at[gy],
            send_sem=h_ss.at[k], recv_sem=h_rs.at[k],
            device_id=(gx, to), device_id_type=MESH,
        )

    def second_copy(k):
        to = lax.rem(gx // 4 + k // 4, 4) * 4 + lax.rem(lax.rem(gx, 4) + k % 4, 4)
        return pltpu.make_async_remote_copy(
            src_ref=h_mid, dst_ref=h_in2.at[gx],
            send_sem=h2_ss.at[k], recv_sem=h2_rs.at[k],
            device_id=(to, gy), device_id_type=MESH,
        )

    for k in range(1, 8):
        first_copy(k).start()
    h_in[gy] = h_send[...]
    mine = owner_v[...] == me
    count = jnp.where(mine, 1.0, 0.0)
    before = jnp.where(
        lax.broadcasted_iota(jnp.int32, (128, 128), 0) < lax.broadcasted_iota(jnp.int32, (128, 128), 1),
        1.0, 0.0,
    )
    above = jnp.where(
        lax.broadcasted_iota(jnp.int32, (8, 8), 1) < lax.broadcasted_iota(jnp.int32, (8, 8), 0),
        1.0, 0.0,
    )
    in_row = jnp.dot(count, before, precision=HIGHEST, preferred_element_type=f32)
    rank = in_row + jnp.dot(
        above, jnp.broadcast_to(jnp.sum(count, axis=1, keepdims=True), (8, 128)),
        precision=HIGHEST, preferred_element_type=f32,
    )
    rank = jnp.where(mine, rank, -1.0)
    for k in range(1, 8):
        first_copy(k).wait_recv()
    total = h_in[0]
    for k in range(1, 8):
        total = total + h_in[k]
    h_mid[...] = total
    for k in range(1, 16):
        second_copy(k).start()
    h_in2[gx] = total
    for k in range(1, 16):
        second_copy(k).wait_recv()
    total = h_in2[0]
    for k in range(1, 16):
        total = total + h_in2[k]

    gain = weights_v[...] * jnp.sqrt(1.0 + total)
    new = 1024.0 * gain / jnp.sum(gain)
    new_o[...] = new
    for k in range(8):
        sens_o[k:k + 1, :] = jnp.broadcast_to(
            jnp.sum(jnp.where(rank == float(k), total, 0.0), keepdims=True), (1, 128)
        )

    ids = ids_v[...]
    lane = lax.broadcasted_iota(jnp.int32, (128, 128), 1)
    picked = jnp.zeros((128, 128), f32)
    for k in range(8):
        picked = picked + jnp.where(ids == lane + k * 128, new_o[k:k + 1, :], 0.0)
    wide[...] = jnp.broadcast_to(jnp.sum(picked, axis=1, keepdims=True), (128, 128))

    def weigh(i, acc):
        for u in range(8):
            slot = i * 8 + u
            acc = acc + wide[pl.ds(slot, 1), :] * dens[slot]
        return acc

    out = lax.fori_loop(0, 16, weigh, jnp.zeros((64, 128), f32))
    dens_o[:, :128] = out[:32]
    dens_o[:, 128:] = out[32:]

    def drain1(pos, c):
        for k in range(4):
            @pl.when(lax.rem(pos, 8) != 3)
            def _():
                copy1(k, pos).wait_send()
        return c

    def drain2(pos, c):
        for k in range(4):
            copy2(k, pos).wait_send()
        return c

    lax.fori_loop(0, 32, drain1, 0)
    lax.fori_loop(0, 24, drain2, 0)
    for k in range(4):
        for of, oc in others:
            meta1(k, of, oc).wait_send()
        for og in (1, 3, 2):
            meta2(k, og).wait_send()
            copy3(k, og).wait_send()
    for k in range(1, 8):
        first_copy(k).wait_send()
    for k in range(1, 16):
        second_copy(k).wait_send()


def local(probes, blk_rows, blk_sensor, blk_count, coef, owner, weights):
    tile_r, tile_c, probe_n = probes.shape
    nblk, foot = blk_rows.shape
    f32, bf16 = jnp.float32, jnp.bfloat16
    alive = jnp.arange(nblk, dtype=jnp.int32) < blk_count[0]
    coef_m = jnp.where(alive[:, None], coef.astype(f32), 0.0)
    rows_t = blk_rows.T.reshape(-1)
    ids = jnp.broadcast_to(blk_sensor.astype(f32)[None, :], (foot, nblk))
    meta = jnp.stack([coef_m.T, ids], axis=1)
    ids_v = jnp.broadcast_to(blk_sensor[:, None], (nblk, 128))
    vmem = pl.BlockSpec(memory_space=pltpu.VMEM)
    smem = pl.BlockSpec(memory_space=pltpu.SMEM)
    dma = pltpu.SemaphoreType.DMA
    sens, new, dens = pl.pallas_call(
        kernel,
        out_shape=(
            jax.ShapeDtypeStruct((8, 128), f32),
            jax.ShapeDtypeStruct((8, 128), f32),
            jax.ShapeDtypeStruct((tile_r, tile_c), f32),
        ),
        in_specs=[smem] + [vmem] * 7,
        out_specs=(vmem, vmem, vmem),
        scratch_shapes=[
            pltpu.VMEM((tile_r * tile_c, 2, 128), f32),
            pltpu.VMEM((3, 256, 128), f32),
            pltpu.VMEM((4, 32, nblk, probe_n), bf16),
            pltpu.VMEM((4, 7, 8, nblk, probe_n), bf16),
            pltpu.VMEM((4, 8, 8, 2, 128), f32),
            pltpu.VMEM((nblk, 64, 128), f32),
            pltpu.VMEM((4, 1024, probe_n), f32),
            pltpu.VMEM((4, 3, 256, probe_n), f32),
            pltpu.VMEM((256, 128), bf16),
            pltpu.VMEM((8, 128), f32),
            pltpu.VMEM((8, 8, 128), f32),
            pltpu.VMEM((8, 128), f32),
            pltpu.VMEM((16, 8, 128), f32),
            pltpu.VMEM((128, 128), f32),
            dma((4, 32)), dma((4, 32)), dma((4, 32)), dma((4, 32)),
            dma((4, 8)), dma((4, 8)), dma((4, 4)), dma((4, 4)),
            dma((4, 4)), dma((4, 4)),
            dma((8,)), dma((8,)), dma((16,)), dma((16,)),
        ],
        compiler_params=pltpu.CompilerParams(
            collective_id=0, has_side_effects=True, vmem_limit_bytes=60 * 2 ** 20
        ),
        name="exchange",
    )(
        rows_t, probes.reshape(tile_r * tile_c, probe_n), meta, blk_rows, coef_m, ids_v,
        owner.reshape(8, 128), weights.reshape(8, 128),
    )
    return sens[:, 0], new.reshape(-1), dens


def solution(mesh):
    in_specs = (
        P("gx", "gy", None),
        P(("gx", "gy"), None),
        P(("gx", "gy")),
        P(("gx", "gy")),
        P(("gx", "gy"), None),
        P(),
        P(),
    )
    out_specs = (P(("gx", "gy")), P(), P("gx", "gy"))
    return jax.shard_map(local, mesh=mesh, in_specs=in_specs, out_specs=out_specs, check_vma=False)
```

time: 160 us -> 127 us (0.79)
  Pallas kernels: 149 us -> 115 us
    pallas_call x1, Pallas kernels: 149 us -> 115 us  [local(): pl.pallas_call(kernel, out_shape=(jax.ShapeDtypeStruct((8, 128), f32), ja...]
where the time goes in v2:
time: 127 us; the launch traced here: 126 us
  Pallas kernels  115 us (91%)
  local copies, waits for them, and re-layouts  7.67 us (6%)
  other arithmetic  2.14 us (2%)
  between operations  1.3 us (1%)
    pallas_call x1, Pallas kernels, local(): pl.pallas_call(kernel, out_shape=(jax.ShapeDtypeStruct((8, 128), f32), ja...  115 us
    unnamed x3, local copies, waits for them, and re-layouts  4.2 us

profile of v2, /device:TPU:1, one launch (start us, length us, event | category | flops | bytes accessed | tf_op | source)
XLA Modules:
  0.0 126.3 jit_solution(11348108184772094097)
XLA Ops:
  1.3 1.5 %convert_select_fusion = (f32[128,128]{1,0:T(8,128)}, f32[128,1,128]{0,2,1:T(8,128)S(1)}) fusion(bf16[128,128]{1,0:T(8,128)(2,1)} %param.11, pred[128]{0:T(512)(128)(4,1)S(1)} %iota_compare_fusion), kind=kLoop, calls=%fused_computation.1 | loop fusion | flops 32768 | bytes 163968 | tf_op jit(solution)/shard_map/jit(_where)/select_n | solution.py:400
  2.8 0.7 convert_element_type.7
  3.4 0.1 stack_broadcast_in_dim.2
  3.5 0.7 copy.12.meta
  4.2 1.6 %copy.11 = s32[128,128]{0,1:T(8,128)} copy(s32[128,128]{1,0:T(8,128)} %rows_v.1) | data formatting | bytes 131072 | tf_op args[1]
  5.8 1.4 %broadcast_in_dim.22.ids_v = s32[128,128]{1,0:T(8,128)} broadcast(s32[128]{0:T(128)} %param.9), dimensions={0} | broadcast | bytes 66048 | tf_op jit(solution)/shard_map/broadcast_in_dim | solution.py:404
  7.2 115.1 %exchange.1 = (f32[8,128]{1,0:T(8,128)}, f32[8,128]{1,0:T(8,128)}, f32[32,256]{1,0:T(8,128)}) custom-call(s32[16384]{0:T(1024)} %bitcast.14, bf16[8192,256]{1,0:T(8,128)(2,1)} %bitcast.13, f32[128,2,128]{2,1,0:T(2,128)} %copy.12.meta, s32[128,128]{1,0:T(8,128)} %rows_v.1, f32[128,128]{1,0:T(8,128)} %get-tuple-element.9.coef_v, ...), custom_call_target="tpu_custom_call" | custom-call | tf_op jit(solution)/shard_map/exchange/pallas_call | solution.py:408
  122.3 1.3 %slice_reduce_fusion = f32[8]{0:T(128)} fusion(f32[8,128]{1,0:T(8,128)} %get-tuple-element.6), kind=kLoop, calls=%fused_computation.2 | loop fusion | bytes 64 | tf_op jit(solution)/shard_map/slice | solution.py:445
  123.6 1.3 %copy.16 = f32[1024]{0:T(1024)} copy(f32[1024]{0:T(1024)} %bitcast.17) | data formatting | bytes 8192
  124.9 1.4 %copy.17 = f32[32,256]{1,0:T(8,128)} copy(f32[32,256]{1,0:T(8,128)} %get-tuple-element.16) | data formatting | bytes 65536
  (2 shorter events, 0.0 us)

commit v3 on v2

v3 whole, which is shorter than its diff:
```python
import jax
import jax.numpy as jnp
from jax import lax
from jax.experimental import pallas as pl
from jax.experimental.pallas import tpu as pltpu
from jax.sharding import PartitionSpec as P

MESH = pl.DeviceIdType.MESH
HIGHEST = lax.Precision.HIGHEST
FIRST = (0, 1, 2, 2)
SECOND = (1, 2, 0, 0)
THIRD = (2, 0, 1, 1)


def place():
    gx, gy = lax.axis_index("gx"), lax.axis_index("gy")
    return [lax.rem(gx, 4), gx // 4, gy // 2], lax.rem(gy, 2)


def peer(axis, off, core_off):
    at, core = place()
    at[axis] = lax.rem(at[axis] + off, 4)
    return at[1] * 4 + at[0], at[2] * 2 + lax.rem(core + core_off, 2)


def order(i):
    return lax.rem(1 + 2 * i - 3 * (i // 2), 4)


def decode(pos):
    return order(pos // 8), order(lax.rem(pos, 4)), lax.rem(pos, 8) // 4


def kernel(
    rows_s, count_v, probes_h, rows_v, coef_b, ids_r, owner_v, weights_v,
    sens_o, new_o, dens_o,
    probes, tile, stage, send, zone, meta, metas, coef_v, ids_v, dens, part, final, steps_v,
    h_send, h_in, h_mid, h_in2, wide,
    in_sem, sent, rs1, rs2, m_sem, fr, h_sem,
):
    n_pts, probe_n = probes.shape
    foot = 128
    chunk = n_pts // 4
    gx, gy = lax.axis_index("gx"), lax.axis_index("gy")
    me = gx * 8 + gy
    at, core = place()
    bf16, f32 = jnp.bfloat16, jnp.float32

    def load(i):
        part_of = pl.ds(i * chunk, chunk)
        return pltpu.make_async_copy(probes_h.at[part_of], probes.at[part_of], in_sem.at[i])

    for i in range(4):
        load(i).start()
    barrier = pltpu.get_barrier_semaphore()

    def greet(device):
        pl.semaphore_signal(barrier, inc=1, device_id=device, device_id_type=MESH)

    for k in range(1, 16):
        greet((lax.rem(gx // 4 + k // 4, 4) * 4 + lax.rem(lax.rem(gx, 4) + k % 4, 4), gy))
    for k in range(1, 8):
        greet((gx, lax.rem(gy + k, 8)))
    for axis in (0, 1):
        for off in (1, 2, 3):
            greet(peer(axis, off, 1))

    flat = tile.reshape(2 * n_pts, 128)

    def widen(i, c):
        block = probes[pl.ds(pl.multiple_of(i * 64, 64), 64), :].astype(f32)
        flat[pl.ds(i * 128, 64, 2), :] = block[:, :128]
        flat[pl.ds(i * 128 + 1, 64, 2), :] = block[:, 128:]
        return c

    slot_of = lax.broadcasted_iota(jnp.int32, (128, 128), 0)
    coef_v[...] = jnp.where(slot_of < count_v[...], coef_b[...].astype(f32), 0.0)
    names_r = jnp.broadcast_to(ids_r[...].astype(f32), (128, 128))
    meta[:, 0, :] = coef_v[...].T
    meta[:, 1, :] = names_r
    ids_v[...] = names_r.T
    for i in range(4):
        load(i).wait()
        lax.fori_loop(i * (chunk // 64), (i + 1) * (chunk // 64), widen, 0)
    for i in range(16):
        steps_v[i * 16:(i + 1) * 16, :] = (
            lax.broadcasted_iota(jnp.int32, (16, 128), 0) + i * 16
        ).astype(f32).astype(bf16)

    def meta1(k, of, oc):
        first = lax.rem(core + oc, 2) * 64 + k * 16 + lax.rem(at[FIRST[k]] + of, 4) * 4
        src = oc * 4 + of
        return pltpu.make_async_remote_copy(
            src_ref=meta.at[pl.ds(first, 4)], dst_ref=metas.at[k, pl.ds(0, 4), src],
            send_sem=m_sem.at[0, k], recv_sem=m_sem.at[1, k],
            device_id=peer(FIRST[k], of, oc), device_id_type=MESH,
        )

    def meta2(k, og):
        return pltpu.make_async_remote_copy(
            src_ref=metas.at[k, lax.rem(at[SECOND[k]] + og, 4)], dst_ref=metas.at[k, 4 + og],
            send_sem=m_sem.at[2, k], recv_sem=m_sem.at[3, k],
            device_id=peer(SECOND[k], og, 0), device_id_type=MESH,
        )

    def copy1(k, pos):
        og, of, oc = decode(pos)
        return pltpu.make_async_remote_copy(
            src_ref=send.at[k, pos], dst_ref=zone.at[k, og + 3 * ((og + 3) // 4), oc * 4 + of],
            send_sem=sent.at[0, k], recv_sem=rs1.at[k, pos // 4],
            device_id=peer(FIRST[k], of, oc), device_id_type=MESH,
        )

    def copy2(k, og, oc):
        return pltpu.make_async_remote_copy(
            src_ref=zone.at[k, 3 + og, oc * 4:oc * 4 + 4], dst_ref=zone.at[k, og, oc * 4:oc * 4 + 4],
            send_sem=sent.at[1, k], recv_sem=rs2.at[k, og * 2 + oc],
            device_id=peer(SECOND[k], og, 0), device_id_type=MESH,
        )

    def await_bytes(ref, sem):
        pltpu.make_async_copy(ref, ref, sem).wait()

    def copy3(k, oh):
        block = lax.rem(at[THIRD[k]] + oh, 4)
        return pltpu.make_async_remote_copy(
            src_ref=part.at[k, pl.ds(pl.multiple_of(block * 256, 256), 256)], dst_ref=final.at[k, oh - 1],
            send_sem=sent.at[2, k], recv_sem=fr.at[k],
            device_id=peer(THIRD[k], oh, 0), device_id_type=MESH,
        )

    others = [(of, oc) for oc in (0, 1) for of in (1, 3, 2, 0) if (of, oc) != (0, 0)]
    for k in range(4):
        metas[k, 0:4, 0] = meta[pl.ds(core * 64 + k * 16 + at[FIRST[k]] * 4, 4)]

    def gather(k, pos, buf):
        og, of, oc = decode(pos)
        chan = (
            lax.rem(core + oc, 2) * 64 + k * 16
            + lax.rem(at[FIRST[k]] + of, 4) * 4 + lax.rem(at[SECOND[k]] + og, 4)
        )
        for i in range(128):
            stage[buf, 2 * i:2 * i + 2, :] = tile[rows_s[chan + i * 128]]
        send[k, pos, :, :128] = stage[buf, pl.ds(0, 128, 2), :].astype(bf16)
        send[k, pos, :, 128:] = stage[buf, pl.ds(1, 128, 2), :].astype(bf16)

    def give(k, pos):
        mine = lax.rem(pos, 8) == 3

        @pl.when(mine)
        def _():
            og, _, _ = decode(pos)
            zone[k, og + 3 * ((og + 3) // 4), 0] = send[k, pos]

        @pl.when(jnp.logical_not(mine))
        def _():
            copy1(k, pos).start()

    def first_loop(pos, c):
        for buf, k in enumerate((2, 0, 1)):
            gather(k, pos, buf)
            if buf == 0:
                @pl.when(pos == 1)
                def _():
                    pl.semaphore_wait(barrier, 28)

            @pl.when(pos > 0)
            def _():
                give(k, pos - 1)

        @pl.when(pos == 2)
        def _():
            for of, oc in others:
                for k in range(4):
                    meta1(k, of, oc).start()
        return c

    lax.fori_loop(0, 32, first_loop, 0)

    def second_loop(pos, c):
        gather(3, pos, 0)

        @pl.when(pos == 0)
        def _():
            for k in (2, 0, 1):
                give(k, 31)

        @pl.when(pos > 0)
        def _():
            give(3, pos - 1)
        return c

    def forward(k, i):
        og = order(i)
        for oc in (0, 1):
            await_bytes(zone.at[k, 3 + og, (1 if oc == 0 else 4):oc * 4 + 4], rs1.at[k, 2 * i + oc])
            copy2(k, og, oc).start()

    forward(2, 0)
    lax.fori_loop(0, 32, second_loop, 0)
    give(3, 31)

    for k in range(4):
        await_bytes(metas.at[k, 0:4, 1:8], m_sem.at[1, k])
    for og in (1, 3, 2):
        for k in range(4):
            meta2(k, og).start()

    q = lax.broadcasted_iota(jnp.int32, (64, 128), 0)
    hi_of = jnp.where(q < 32, 2 * q, 2 * q - 63)
    lo_of = lax.broadcasted_iota(jnp.int32, (128, 128), 0)

    def spread(first):
        for u in range(4):
            row = rows_v[pl.ds(first + u, 1), :]
            val = coef_v[pl.ds(first + u, 1), :]
            high = jnp.where(row // 128 == hi_of, val, 0.0).astype(bf16)
            low = jnp.where(lax.rem(row, 128) == lo_of, val, 0.0).astype(bf16)
            dens[first + u] = lax.dot_general(
                high, low, (((1,), (1,)), ((), ())), preferred_element_type=f32
            )

    def spread_loop(i, c):
        spread(i * 4)
        return c

    forward(2, 1)
    forward(0, 0)
    forward(1, 0)
    lax.fori_loop(0, 12, spread_loop, 0)
    for k in (0, 2, 1):
        if k != 2:
            forward(k, 1)
        forward(k, 2)
    lax.fori_loop(12, 24, spread_loop, 0)
    part[...] = jnp.zeros_like(part)

    def mix(k, group):
        og, oc = order(group // 2), lax.rem(group, 2)

        @pl.when(group < 6)
        def _():
            await_bytes(zone.at[k, og, pl.ds(oc * 4, 4)], rs2.at[k, og * 2 + oc])

        @pl.when(group == 6)
        def _():
            await_bytes(zone.at[k, 0, 1:4], rs1.at[k, 6])

        @pl.when(group == 7)
        def _():
            await_bytes(zone.at[k, 0, 4:8], rs1.at[k, 7])

        cols = zone[k, og, pl.ds(oc * 4, 4)].reshape(512, probe_n)
        slot = og + 4 * ((og + 3) // 4) + at[SECOND[k]] * (1 - (og + 3) // 4)
        tags = [metas[k, slot, oc * 4 + u] for u in range(4)]
        vals = [jnp.broadcast_to(t[0:1], (16, 128)).astype(bf16) for t in tags]
        zero = jnp.zeros((16, 128), bf16)
        for m in range(4):
            names = [jnp.broadcast_to(t[1:2] - float(m * 256), (16, 128)).astype(bf16) for t in tags]
            mixer = jnp.concatenate(
                [
                    jnp.concatenate(
                        [
                            jnp.where(names[u] == steps_v[i * 16:(i + 1) * 16, :], vals[u], zero)
                            for i in range(16)
                        ],
                        axis=0,
                    )
                    for u in range(4)
                ],
                axis=1,
            )
            part[k, m * 256:(m + 1) * 256, :] += jnp.dot(mixer, cols, preferred_element_type=f32)

    for k in range(4):
        await_bytes(metas.at[k, 5:8], m_sem.at[3, k])
    for i in range(3):
        spread(96 + i * 8)
        spread(100 + i * 8)
        mix(0, 6 + i if i < 2 else 0)
        forward(3, i)
    spread(120)
    spread(124)

    def mix_loop(*kinds):
        def body(i, c):
            for k in kinds:
                mix(k, lax.rem(i + 6, 8))
            return c
        return body

    lax.fori_loop(3, 8, mix_loop(0), 0)
    for oh in (1, 3, 2):
        copy3(0, oh).start()
    lax.fori_loop(0, 8, mix_loop(2), 0)
    for oh in (1, 3, 2):
        copy3(2, oh).start()
    lax.fori_loop(0, 8, mix_loop(1, 3), 0)
    for k in (1, 3):
        for oh in (1, 3, 2):
            copy3(k, oh).start()

    h_send[...] = jnp.zeros_like(h_send)
    ones = jnp.ones((8, 128), f32)
    for k in (0, 2, 1, 3):
        await_bytes(final.at[k], fr.at[k])
        block = at[THIRD[k]]
        whole = part[k, pl.ds(pl.multiple_of(block * 256, 256), 256), :]
        for i in range(3):
            whole = whole + final[k, i]
        whole = whole * whole
        sums = lax.dot_general(
            ones, whole[:, :128] + whole[:, 128:], (((1,), (1,)), ((), ())),
            preferred_element_type=f32, precision=HIGHEST,
        ) * (1.0 / (foot * probe_n))
        for i in range(2):
            h_send[pl.ds(2 * block + i, 1), :] += sums[0:1, i * 128:(i + 1) * 128]

    def first_copy(k):
        to = lax.rem(gy + k, 8)
        return pltpu.make_async_remote_copy(
            src_ref=h_send, dst_ref=h_in.at[gy],
            send_sem=h_sem.at[0], recv_sem=h_sem.at[1],
            device_id=(gx, to), device_id_type=MESH,
        )

    def second_copy(k):
        to = lax.rem(gx // 4 + k // 4, 4) * 4 + lax.rem(lax.rem(gx, 4) + k % 4, 4)
        return pltpu.make_async_remote_copy(
            src_ref=h_mid, dst_ref=h_in2.at[gx],
            send_sem=h_sem.at[2], recv_sem=h_sem.at[3],
            device_id=(to, gy), device_id_type=MESH,
        )

    for k in range(1, 8):
        first_copy(k).start()
    h_in[gy] = h_send[...]
    mine = owner_v[...] == me
    count = jnp.where(mine, 1.0, 0.0)
    before = jnp.where(
        lax.broadcasted_iota(jnp.int32, (128, 128), 0) < lax.broadcasted_iota(jnp.int32, (128, 128), 1),
        1.0, 0.0,
    )
    above = jnp.where(
        lax.broadcasted_iota(jnp.int32, (8, 8), 1) < lax.broadcasted_iota(jnp.int32, (8, 8), 0),
        1.0, 0.0,
    )
    in_row = jnp.dot(count, before, precision=HIGHEST, preferred_element_type=f32)
    rank = in_row + jnp.dot(
        above, jnp.broadcast_to(jnp.sum(count, axis=1, keepdims=True), (8, 128)),
        precision=HIGHEST, preferred_element_type=f32,
    )
    rank = jnp.where(mine, rank, -1.0)
    await_bytes(h_in.at[1:8], h_sem.at[1])
    total = h_in[0]
    for k in range(1, 8):
        total = total + h_in[k]
    h_mid[...] = total
    for k in range(1, 16):
        second_copy(k).start()
    h_in2[gx] = total
    await_bytes(h_in2.at[1:16], h_sem.at[3])
    total = h_in2[0]
    for k in range(1, 16):
        total = total + h_in2[k]

    gain = weights_v[...] * jnp.sqrt(1.0 + total)
    new = 1024.0 * gain / jnp.sum(gain)
    new_o[...] = new
    for k in range(8):
        sens_o[k] = jnp.sum(jnp.where(rank == float(k), total, 0.0))

    ids = ids_v[...]
    lane = lax.broadcasted_iota(jnp.int32, (128, 128), 1)
    picked = jnp.zeros((128, 128), f32)
    for k in range(8):
        picked = picked + jnp.where(ids == (lane + k * 128).astype(f32), new_o[k:k + 1, :], 0.0)
    wide[...] = jnp.broadcast_to(jnp.sum(picked, axis=1, keepdims=True), (128, 128))

    def weigh(i, acc):
        for u in range(8):
            slot = i * 8 + u
            acc = acc + wide[pl.ds(slot, 1), :] * dens[slot]
        return acc

    out = lax.fori_loop(0, 16, weigh, jnp.zeros((64, 128), f32))
    dens_o[:, :128] = out[:32]
    dens_o[:, 128:] = out[32:]

    for k in range(4):
        await_bytes(send.at[k, 0:28], sent.at[0, k])
        await_bytes(zone.at[k, 1:4], sent.at[1, k])
        await_bytes(final.at[k], sent.at[2, k])
        await_bytes(metas.at[k, 0:4, 1:8], m_sem.at[0, k])
        await_bytes(metas.at[k, 5:8], m_sem.at[2, k])
    await_bytes(h_in.at[1:8], h_sem.at[0])
    await_bytes(h_in2.at[1:16], h_sem.at[2])


def finish(sens, new, dens, sens_o, new_o, dens_o):
    for k in range(8):
        sens_o[k] = sens[k]
    new_o[...] = new[...]
    dens_o[...] = dens[...]


def local(probes, blk_rows, blk_sensor, blk_count, coef, owner, weights):
    tile_r, tile_c, probe_n = probes.shape
    nblk, foot = blk_rows.shape
    f32, bf16 = jnp.float32, jnp.bfloat16
    vmem = pl.BlockSpec(memory_space=pltpu.VMEM)
    smem = pl.BlockSpec(memory_space=pltpu.SMEM)
    anyw = pl.BlockSpec(memory_space=pl.ANY)
    dma = pltpu.SemaphoreType.DMA
    outs = (
        jax.ShapeDtypeStruct((8,), f32),
        jax.ShapeDtypeStruct((8, 128), f32),
        jax.ShapeDtypeStruct((tile_r, tile_c), f32),
    )
    sens, new, dens = pl.pallas_call(
        kernel,
        out_shape=outs,
        in_specs=[smem, vmem, anyw] + [vmem] * 5,
        out_specs=(smem, vmem, vmem),
        scratch_shapes=[
            pltpu.VMEM((tile_r * tile_c, probe_n), bf16),
            pltpu.VMEM((tile_r * tile_c, 2, 128), f32),
            pltpu.VMEM((3, 256, 128), f32),
            pltpu.VMEM((4, 32, nblk, probe_n), bf16),
            pltpu.VMEM((4, 7, 8, nblk, probe_n), bf16),
            pltpu.VMEM((128, 2, 128), f32),
            pltpu.VMEM((4, 8, 8, 2, 128), f32),
            pltpu.VMEM((nblk, foot), f32),
            pltpu.VMEM((nblk, foot), f32),
            pltpu.VMEM((nblk, 64, 128), f32),
            pltpu.VMEM((4, 1024, probe_n), f32),
            pltpu.VMEM((4, 3, 256, probe_n), f32),
            pltpu.VMEM((256, 128), bf16),
            pltpu.VMEM((8, 128), f32),
            pltpu.VMEM((8, 8, 128), f32),
            pltpu.VMEM((8, 128), f32),
            pltpu.VMEM((16, 8, 128), f32),
            pltpu.VMEM((128, 128), f32),
            dma((4,)), dma((3, 4)), dma((4, 8)), dma((4, 8)), dma((4, 4)), dma((4,)), dma((4,)),
        ],
        compiler_params=pltpu.CompilerParams(
            collective_id=0, has_side_effects=True, vmem_limit_bytes=60 * 2 ** 20
        ),
        name="exchange",
    )(
        blk_rows.reshape(-1), blk_count.reshape(1, 1), probes.reshape(tile_r * tile_c, probe_n), blk_rows, coef,
        blk_sensor.reshape(1, nblk), owner.reshape(8, 128), weights.reshape(8, 128),
    )
    sens, new, dens = pl.pallas_call(
        finish, out_shape=outs, in_specs=[smem, vmem, vmem], out_specs=(smem, vmem, vmem), name="finish",
    )(sens, new, dens)
    return sens, new.reshape(-1), dens


def solution(mesh):
    in_specs = (
        P("gx", "gy", None),
        P(("gx", "gy"), None),
        P(("gx", "gy")),
        P(("gx", "gy")),
        P(("gx", "gy"), None),
        P(),
        P(),
    )
    out_specs = (P(("gx", "gy")), P(), P("gx", "gy"))
    return jax.shard_map(local, mesh=mesh, in_specs=in_specs, out_specs=out_specs, check_vma=False)
```

time: 127 us -> 114 us (0.90)
  local copies, waits for them, and re-layouts: 7.67 us -> 0 us
  other arithmetic: 2.14 us -> 0 us
  Pallas kernels: 115 us -> 113 us
    unnamed x3 -> x0, local copies, waits for them, and re-layouts: 4.2 us -> none
    pallas_call x1 -> x2, Pallas kernels: 115 us -> 113 us  [the longest x1 111 us: local(): pl.pallas_call(kernel, out_shape=outs, in_specs=[smem, vmem, anyw] + [vme...]
    select_n x1 -> x0, other arithmetic: 1.46 us -> none  [local(): coef_m = jnp.where(alive[:, None], coef.astype(f32), 0.0)]
    broadcast_in_dim x1 -> x0, local copies, waits for them, and re-layouts: 1.35 us -> none  [local(): ids_v = jnp.broadcast_to(blk_sensor[:, None], (nblk, 128))]
    slice x1 -> x0, local copies, waits for them, and re-layouts: 1.3 us -> none  [local(): return (sens[:, 0], new.reshape(-1), dens)]
where the time goes in v3:
time: 114 us
  Pallas kernels  113 us (99%)
  between operations  1.29 us (1%)
    pallas_call x1, Pallas kernels, local(): pl.pallas_call(kernel, out_shape=outs, in_specs=[smem, vmem, anyw] + [vme...  111 us

profile of v3, /device:TPU:1, one launch (start us, length us, event | category | flops | bytes accessed | tf_op | source)
XLA Modules:
  0.0 113.9 jit_solution(12457698980629398582)
XLA Ops:
  1.3 111.2 %exchange.1 = (f32[8]{0:T(128)}, f32[8,128]{1,0:T(8,128)}, f32[32,256]{1,0:T(8,128)}) custom-call(s32[16384]{0:T(1024)} %bitcast.9, s32[1,1]{1,0:T(1,128)} %bitcast.7.count_v, bf16[8192,256]{1,0:T(8,128)(2,1)} %bitcast.8, s32[128,128]{1,0:T(8,128)} %rows_v.1, bf16[128,128]{1,0:T(8,128)(2,1)} %coef_b.1, s32[1,128]{1,0:T(1,128)} %bitcast.12, ...), custom_call_target="tpu_custom_call" | custom-call | tf_op jit(solution)/shard_map/exchange/pallas_call | solution.py:420
  112.5 1.4 %finish.1 = (f32[8]{0:T(128)}, f32[8,128]{1,0:T(8,128)}, f32[32,256]{1,0:T(8,128)}) custom-call(f32[8]{0:T(128)} %get-tuple-element.9.sens, f32[8,128]{1,0:T(8,128)} %get-tuple-element.10.new, f32[32,256]{1,0:T(8,128)} %get-tuple-element.11.dens), custom_call_target="tpu_custom_call" | custom-call | tf_op jit(solution)/shard_map/finish/pallas_call | solution.py:454

commit v4 on v3

--- a/solution.py
+++ b/solution.py
@@ -32,11 +32,11 @@
 
 
 def kernel(
-    rows_s, count_v, probes_h, rows_v, coef_b, ids_r, owner_v, weights_v,
+    rows_h, count_v, probes_h, rows_v, coef_b, ids_r, owner_v, weights_v,
     sens_o, new_o, dens_o,
-    probes, tile, stage, send, zone, meta, metas, coef_v, ids_v, dens, part, final, steps_v,
+    rows_s, probes, tile, stage, send, zone, meta, metas, coef_v, ids_v, dens, part, final, steps_v,
     h_send, h_in, h_mid, h_in2, wide,
-    in_sem, sent, rs1, rs2, m_sem, fr, h_sem,
+    in_sem, row_sem, sent, rs1, rs2, m_sem, fr, h_sem,
 ):
     n_pts, probe_n = probes.shape
     foot = 128
@@ -50,8 +50,10 @@
         part_of = pl.ds(i * chunk, chunk)
         return pltpu.make_async_copy(probes_h.at[part_of], probes.at[part_of], in_sem.at[i])
 
+    rows_in = pltpu.make_async_copy(rows_h, rows_s, row_sem)
     for i in range(4):
         load(i).start()
+    rows_in.start()
     barrier = pltpu.get_barrier_semaphore()
 
     def greet(device):
@@ -82,6 +84,7 @@
     for i in range(4):
         load(i).wait()
         lax.fori_loop(i * (chunk // 64), (i + 1) * (chunk // 64), widen, 0)
+    rows_in.wait()
     for i in range(16):
         steps_v[i * 16:(i + 1) * 16, :] = (
             lax.broadcasted_iota(jnp.int32, (16, 128), 0) + i * 16
@@ -156,55 +159,61 @@
         def _():
             copy1(k, pos).start()
 
+    def forward(k, i):
+        og = order(i)
+        for oc in (0, 1):
+            await_bytes(zone.at[k, 3 + og, (1 if oc == 0 else 4):oc * 4 + 4], rs1.at[k, 2 * i + oc])
+            copy2(k, og, oc).start()
+
     def first_loop(pos, c):
-        for buf, k in enumerate((2, 0, 1)):
+        for buf, k in enumerate((2, 0)):
             gather(k, pos, buf)
             if buf == 0:
                 @pl.when(pos == 1)
                 def _():
                     pl.semaphore_wait(barrier, 28)
+                    for of, oc in others:
+                        for j in range(4):
+                            meta1(j, of, oc).start()
+
+                @pl.when(pos == 16)
+                def _():
+                    for j in range(4):
+                        await_bytes(metas.at[j, 0:4, 1:8], m_sem.at[1, j])
+                    for og in (1, 3, 2):
+                        for j in range(4):
+                            meta2(j, og).start()
 
             @pl.when(pos > 0)
             def _():
                 give(k, pos - 1)
 
-        @pl.when(pos == 2)
-        def _():
-            for of, oc in others:
-                for k in range(4):
-                    meta1(k, of, oc).start()
         return c
 
+    def second_loop(pos, c):
+        for buf, k in enumerate((3, 1)):
+            gather(k, pos, buf)
+            if buf == 0:
+                @pl.when(pos == 0)
+                def _():
+                    for j in (2, 0):
+                        give(j, 31)
+
+                @pl.when(pos == 16)
+                def _():
+                    forward(2, 1)
+
+            @pl.when(pos > 0)
+            def _():
+                give(k, pos - 1)
+
+        return c
+
     lax.fori_loop(0, 32, first_loop, 0)
-
-    def second_loop(pos, c):
-        gather(3, pos, 0)
-
-        @pl.when(pos == 0)
-        def _():
-            for k in (2, 0, 1):
-                give(k, 31)
-
-        @pl.when(pos > 0)
-        def _():
-            give(3, pos - 1)
-        return c
-
-    def forward(k, i):
-        og = order(i)
-        for oc in (0, 1):
-            await_bytes(zone.at[k, 3 + og, (1 if oc == 0 else 4):oc * 4 + 4], rs1.at[k, 2 * i + oc])
-            copy2(k, og, oc).start()
-
     forward(2, 0)
     lax.fori_loop(0, 32, second_loop, 0)
     give(3, 31)
-
-    for k in range(4):
-        await_bytes(metas.at[k, 0:4, 1:8], m_sem.at[1, k])
-    for og in (1, 3, 2):
-        for k in range(4):
-            meta2(k, og).start()
+    give(1, 31)
 
     q = lax.broadcasted_iota(jnp.int32, (64, 128), 0)
     hi_of = jnp.where(q < 32, 2 * q, 2 * q - 63)
@@ -223,17 +232,6 @@
     def spread_loop(i, c):
         spread(i * 4)
         return c
-
-    forward(2, 1)
-    forward(0, 0)
-    forward(1, 0)
-    lax.fori_loop(0, 12, spread_loop, 0)
-    for k in (0, 2, 1):
-        if k != 2:
-            forward(k, 1)
-        forward(k, 2)
-    lax.fori_loop(12, 24, spread_loop, 0)
-    part[...] = jnp.zeros_like(part)
 
     def mix(k, group):
         og, oc = order(group // 2), lax.rem(group, 2)
@@ -272,16 +270,6 @@
             )
             part[k, m * 256:(m + 1) * 256, :] += jnp.dot(mixer, cols, preferred_element_type=f32)
 
-    for k in range(4):
-        await_bytes(metas.at[k, 5:8], m_sem.at[3, k])
-    for i in range(3):
-        spread(96 + i * 8)
-        spread(100 + i * 8)
-        mix(0, 6 + i if i < 2 else 0)
-        forward(3, i)
-    spread(120)
-    spread(124)
-
     def mix_loop(*kinds):
         def body(i, c):
             for k in kinds:
@@ -289,20 +277,37 @@
             return c
         return body
 
-    lax.fori_loop(3, 8, mix_loop(0), 0)
-    for oh in (1, 3, 2):
-        copy3(0, oh).start()
-    lax.fori_loop(0, 8, mix_loop(2), 0)
-    for oh in (1, 3, 2):
-        copy3(2, oh).start()
-    lax.fori_loop(0, 8, mix_loop(1, 3), 0)
-    for k in (1, 3):
+    def sum_up(k):
         for oh in (1, 3, 2):
             copy3(k, oh).start()
 
+    forward(2, 2)
+    for i in range(3):
+        forward(0, i)
+    forward(1, 0)
+    part[...] = jnp.zeros_like(part)
+    for k in range(4):
+        await_bytes(metas.at[k, 5:8], m_sem.at[3, k])
+    lax.fori_loop(0, 16, spread_loop, 0)
+    forward(3, 0)
+    forward(1, 1)
+    lax.fori_loop(16, 32, spread_loop, 0)
+    lax.fori_loop(0, 4, mix_loop(2), 0)
+    forward(1, 2)
+    forward(3, 1)
+    lax.fori_loop(4, 8, mix_loop(2), 0)
+    sum_up(2)
+    lax.fori_loop(0, 4, mix_loop(0), 0)
+    forward(3, 2)
+    lax.fori_loop(4, 8, mix_loop(0), 0)
+    sum_up(0)
+    lax.fori_loop(0, 8, mix_loop(1, 3), 0)
+    sum_up(1)
+    sum_up(3)
+
     h_send[...] = jnp.zeros_like(h_send)
     ones = jnp.ones((8, 128), f32)
-    for k in (0, 2, 1, 3):
+    for k in (2, 0, 1, 3):
         await_bytes(final.at[k], fr.at[k])
         block = at[THIRD[k]]
         whole = part[k, pl.ds(pl.multiple_of(block * 256, 256), 256), :]
@@ -420,9 +425,10 @@
     sens, new, dens = pl.pallas_call(
         kernel,
         out_shape=outs,
-        in_specs=[smem, vmem, anyw] + [vmem] * 5,
+        in_specs=[anyw, vmem, anyw] + [vmem] * 5,
         out_specs=(smem, vmem, vmem),
         scratch_shapes=[
+            pltpu.SMEM((nblk * foot,), jnp.int32),
             pltpu.VMEM((tile_r * tile_c, probe_n), bf16),
             pltpu.VMEM((tile_r * tile_c, 2, 128), f32),
             pltpu.VMEM((3, 256, 128), f32),
@@ -441,7 +447,7 @@
             pltpu.VMEM((8, 128), f32),
             pltpu.VMEM((16, 8, 128), f32),
             pltpu.VMEM((128, 128), f32),
-            dma((4,)), dma((3, 4)), dma((4, 8)), dma((4, 8)), dma((4, 4)), dma((4,)), dma((4,)),
+            dma((4,)), dma(()), dma((3, 4)), dma((4, 8)), dma((4, 8)), dma((4, 4)), dma((4,)), dma((4,)),
         ],
         compiler_params=pltpu.CompilerParams(
             collective_id=0, has_side_effects=True, vmem_limit_bytes=60 * 2 ** 20

time: 114 us -> 108 us (0.947)
  Pallas kernels: 113 us -> 107 us
    pallas_call x1, Pallas kernels: 111 us -> 105 us  [local(): pl.pallas_call(kernel, out_shape=outs, in_specs=[anyw, vmem, anyw] + [vme...]
where the time goes in v4:
time: 108 us
  Pallas kernels  107 us (99%)
  between operations  1.29 us (1%)
    pallas_call x1, Pallas kernels, local(): pl.pallas_call(kernel, out_shape=outs, in_specs=[anyw, vmem, anyw] + [vme...  105 us

profile of v4, /device:TPU:1, one launch (start us, length us, event | category | flops | bytes accessed | tf_op | source)
XLA Modules:
  0.0 107.9 jit_solution(9827036770217112644)
XLA Ops:
  1.3 105.2 %exchange.1 = (f32[8]{0:T(128)}, f32[8,128]{1,0:T(8,128)}, f32[32,256]{1,0:T(8,128)}) custom-call(s32[16384]{0:T(1024)} %bitcast.9, s32[1,1]{1,0:T(1,128)} %bitcast.7.count_v, bf16[8192,256]{1,0:T(8,128)(2,1)} %bitcast.8, s32[128,128]{1,0:T(8,128)} %rows_v.1, bf16[128,128]{1,0:T(8,128)(2,1)} %coef_b.1, s32[1,128]{1,0:T(1,128)} %bitcast.12, ...), custom_call_target="tpu_custom_call" | custom-call | tf_op jit(solution)/shard_map/exchange/pallas_call | solution.py:425
  106.5 1.4 %finish.1 = (f32[8]{0:T(128)}, f32[8,128]{1,0:T(8,128)}, f32[32,256]{1,0:T(8,128)}) custom-call(f32[8]{0:T(128)} %get-tuple-element.9.sens, f32[8,128]{1,0:T(8,128)} %get-tuple-element.10.new, f32[32,256]{1,0:T(8,128)} %get-tuple-element.11.dens), custom_call_target="tpu_custom_call" | custom-call | tf_op jit(solution)/shard_map/finish/pallas_call | solution.py:460

commit v5 on v4

--- a/solution.py
+++ b/solution.py
@@ -34,7 +34,7 @@
 def kernel(
     rows_h, count_v, probes_h, rows_v, coef_b, ids_r, owner_v, weights_v,
     sens_o, new_o, dens_o,
-    rows_s, probes, tile, stage, send, zone, meta, metas, coef_v, ids_v, dens, part, final, steps_v,
+    rows_s, probes, tile, stage, send, zone, meta, metas, coef_v, ids_v, dens, part, parcel, final, dither, steps_v,
     h_send, h_in, h_mid, h_in2, wide,
     in_sem, row_sem, sent, rs1, rs2, m_sem, fr, h_sem,
 ):
@@ -84,6 +84,13 @@
     for i in range(4):
         load(i).wait()
         lax.fori_loop(i * (chunk // 64), (i + 1) * (chunk // 64), widen, 0)
+    level = (
+        lax.rem(lax.broadcasted_iota(jnp.int32, (8, probe_n), 1) * 97, probe_n).astype(f32) + 0.5
+    ) * (1.0 / probe_n)
+    bell = jnp.where(
+        level < 0.5, jnp.sqrt(2.0 * level) - 1.0, 1.0 - jnp.sqrt(jnp.maximum(2.0 - 2.0 * level, 0.0))
+    )
+    dither[...] = 1.0 + bell * (1.0 / 128)
     rows_in.wait()
     for i in range(16):
         steps_v[i * 16:(i + 1) * 16, :] = (
@@ -125,9 +132,8 @@
         pltpu.make_async_copy(ref, ref, sem).wait()
 
     def copy3(k, oh):
-        block = lax.rem(at[THIRD[k]] + oh, 4)
-        return pltpu.make_async_remote_copy(
-            src_ref=part.at[k, pl.ds(pl.multiple_of(block * 256, 256), 256)], dst_ref=final.at[k, oh - 1],
+        return pltpu.make_async_remote_copy(
+            src_ref=parcel.at[k, oh - 1], dst_ref=final.at[k, oh - 1],
             send_sem=sent.at[2, k], recv_sem=fr.at[k],
             device_id=peer(THIRD[k], oh, 0), device_id_type=MESH,
         )
@@ -278,6 +284,10 @@
         return body
 
     def sum_up(k):
+        for oh in (1, 3, 2):
+            block = lax.rem(at[THIRD[k]] + oh, 4)
+            rows = part[k, pl.ds(pl.multiple_of(block * 256, 256), 256), :]
+            parcel[k, oh - 1] = (rows * dither[0:1, :]).astype(bf16)
         for oh in (1, 3, 2):
             copy3(k, oh).start()
 
@@ -312,7 +322,7 @@
         block = at[THIRD[k]]
         whole = part[k, pl.ds(pl.multiple_of(block * 256, 256), 256), :]
         for i in range(3):
-            whole = whole + final[k, i]
+            whole = whole + final[k, i].astype(f32)
         whole = whole * whole
         sums = lax.dot_general(
             ones, whole[:, :128] + whole[:, 128:], (((1,), (1,)), ((), ())),
@@ -440,7 +450,9 @@
             pltpu.VMEM((nblk, foot), f32),
             pltpu.VMEM((nblk, 64, 128), f32),
             pltpu.VMEM((4, 1024, probe_n), f32),
-            pltpu.VMEM((4, 3, 256, probe_n), f32),
+            pltpu.VMEM((4, 3, 256, probe_n), bf16),
+            pltpu.VMEM((4, 3, 256, probe_n), bf16),
+            pltpu.VMEM((8, probe_n), f32),
             pltpu.VMEM((256, 128), bf16),
             pltpu.VMEM((8, 128), f32),
             pltpu.VMEM((8, 8, 128), f32),

time: 108 us -> 103 us (0.954)
  Pallas kernels: 107 us -> 101 us
    pallas_call x1, Pallas kernels: 105 us -> 99.7 us  [local(): pl.pallas_call(kernel, out_shape=outs, in_specs=[anyw, vmem, anyw] + [vme...]
where the time goes in v5:
time: 103 us; the launch traced here: 102 us
  Pallas kernels  101 us (98%)
  between operations  1.29 us (1%)
    pallas_call x1, Pallas kernels, local(): pl.pallas_call(kernel, out_shape=outs, in_specs=[anyw, vmem, anyw] + [vme...  99.7 us

profile of v5, /device:TPU:1, one launch (start us, length us, event | category | flops | bytes accessed | tf_op | source)
XLA Modules:
  0.0 102.4 jit_solution(13724326377496181827)
XLA Ops:
  1.3 99.7 %exchange.1 = (f32[8]{0:T(128)}, f32[8,128]{1,0:T(8,128)}, f32[32,256]{1,0:T(8,128)}) custom-call(s32[16384]{0:T(1024)} %bitcast.9, s32[1,1]{1,0:T(1,128)} %bitcast.7.count_v, bf16[8192,256]{1,0:T(8,128)(2,1)} %bitcast.8, s32[128,128]{1,0:T(8,128)} %rows_v.1, bf16[128,128]{1,0:T(8,128)(2,1)} %coef_b.1, s32[1,128]{1,0:T(1,128)} %bitcast.12, ...), custom_call_target="tpu_custom_call" | custom-call | tf_op jit(solution)/shard_map/exchange/pallas_call | solution.py:435
  101.0 1.4 %finish.1 = (f32[8]{0:T(128)}, f32[8,128]{1,0:T(8,128)}, f32[32,256]{1,0:T(8,128)}) custom-call(f32[8]{0:T(128)} %get-tuple-element.9.sens, f32[8,128]{1,0:T(8,128)} %get-tuple-element.10.new, f32[32,256]{1,0:T(8,128)} %get-tuple-element.11.dens), custom_call_target="tpu_custom_call" | custom-call | tf_op jit(solution)/shard_map/finish/pallas_call | solution.py:472

commit v6 on v5

--- a/solution.py
+++ b/solution.py
@@ -7,9 +7,10 @@
 
 MESH = pl.DeviceIdType.MESH
 HIGHEST = lax.Precision.HIGHEST
-FIRST = (0, 1, 2, 2)
-SECOND = (1, 2, 0, 0)
-THIRD = (2, 0, 1, 1)
+FIRST = (0, 1, 2, 0)
+SECOND = (1, 2, 0, 1)
+THIRD = (2, 0, 1, 2)
+TURN = {2: 0, 1: 1, 3: 2, 0: 3}
 
 
 def place():
@@ -28,15 +29,17 @@
 
 
 def decode(pos):
-    return order(pos // 8), order(lax.rem(pos, 4)), lax.rem(pos, 8) // 4
+    a, b = lax.rem(pos // 8, 2), pos // 16
+    return 2 - a + b - 2 * a * b, order(lax.rem(pos, 4)), lax.rem(pos, 8) // 4
 
 
 def kernel(
     rows_h, count_v, probes_h, rows_v, coef_b, ids_r, owner_v, weights_v,
     sens_o, new_o, dens_o,
-    rows_s, probes, tile, stage, send, zone, meta, metas, coef_v, ids_v, dens, part, parcel, final, dither, steps_v,
+    rows_s, probes, tile, stage, send, zone, meta, metas, coef_v, ids_v, dens, part,
+    out1, in1, out2, in2, parcel, final, dither, steps_v,
     h_send, h_in, h_mid, h_in2, wide,
-    in_sem, row_sem, sent, rs1, rs2, m_sem, fr, h_sem,
+    in_sem, row_sem, sent, rs1, r1_sem, r2_sem, m_sem, fr, h_sem,
 ):
     n_pts, probe_n = probes.shape
     foot = 128
@@ -106,26 +109,26 @@
             device_id=peer(FIRST[k], of, oc), device_id_type=MESH,
         )
 
-    def meta2(k, og):
-        return pltpu.make_async_remote_copy(
-            src_ref=metas.at[k, lax.rem(at[SECOND[k]] + og, 4)], dst_ref=metas.at[k, 4 + og],
-            send_sem=m_sem.at[2, k], recv_sem=m_sem.at[3, k],
-            device_id=peer(SECOND[k], og, 0), device_id_type=MESH,
-        )
-
     def copy1(k, pos):
         og, of, oc = decode(pos)
         return pltpu.make_async_remote_copy(
-            src_ref=send.at[k, pos], dst_ref=zone.at[k, og + 3 * ((og + 3) // 4), oc * 4 + of],
+            src_ref=send.at[k, pos], dst_ref=zone.at[k, og, oc * 4 + of],
             send_sem=sent.at[0, k], recv_sem=rs1.at[k, pos // 4],
             device_id=peer(FIRST[k], of, oc), device_id_type=MESH,
         )
 
-    def copy2(k, og, oc):
-        return pltpu.make_async_remote_copy(
-            src_ref=zone.at[k, 3 + og, oc * 4:oc * 4 + 4], dst_ref=zone.at[k, og, oc * 4:oc * 4 + 4],
-            send_sem=sent.at[1, k], recv_sem=rs2.at[k, og * 2 + oc],
-            device_id=peer(SECOND[k], og, 0), device_id_type=MESH,
+    def ring1(k, half):
+        return pltpu.make_async_remote_copy(
+            src_ref=out1.at[k, half], dst_ref=in1.at[k, half],
+            send_sem=sent.at[1, k], recv_sem=r1_sem.at[k, half],
+            device_id=peer(SECOND[k], 1 + 2 * half, 0), device_id_type=MESH,
+        )
+
+    def ring2(k, half):
+        return pltpu.make_async_remote_copy(
+            src_ref=out2.at[k, half], dst_ref=in2.at[k, half],
+            send_sem=sent.at[3, k], recv_sem=r2_sem.at[k, half],
+            device_id=peer(SECOND[k], 1 + 2 * half, 0), device_id_type=MESH,
         )
 
     def await_bytes(ref, sem):
@@ -159,20 +162,14 @@
         @pl.when(mine)
         def _():
             og, _, _ = decode(pos)
-            zone[k, og + 3 * ((og + 3) // 4), 0] = send[k, pos]
+            zone[k, og, 0] = send[k, pos]
 
         @pl.when(jnp.logical_not(mine))
         def _():
             copy1(k, pos).start()
 
-    def forward(k, i):
-        og = order(i)
-        for oc in (0, 1):
-            await_bytes(zone.at[k, 3 + og, (1 if oc == 0 else 4):oc * 4 + 4], rs1.at[k, 2 * i + oc])
-            copy2(k, og, oc).start()
-
     def first_loop(pos, c):
-        for buf, k in enumerate((2, 0)):
+        for buf, k in enumerate((2, 0, 1)):
             gather(k, pos, buf)
             if buf == 0:
                 @pl.when(pos == 1)
@@ -182,14 +179,6 @@
                         for j in range(4):
                             meta1(j, of, oc).start()
 
-                @pl.when(pos == 16)
-                def _():
-                    for j in range(4):
-                        await_bytes(metas.at[j, 0:4, 1:8], m_sem.at[1, j])
-                    for og in (1, 3, 2):
-                        for j in range(4):
-                            meta2(j, og).start()
-
             @pl.when(pos > 0)
             def _():
                 give(k, pos - 1)
@@ -197,29 +186,13 @@
         return c
 
     def second_loop(pos, c):
-        for buf, k in enumerate((3, 1)):
-            gather(k, pos, buf)
-            if buf == 0:
-                @pl.when(pos == 0)
-                def _():
-                    for j in (2, 0):
-                        give(j, 31)
-
-                @pl.when(pos == 16)
-                def _():
-                    forward(2, 1)
-
-            @pl.when(pos > 0)
-            def _():
-                give(k, pos - 1)
+        gather(3, pos, 0)
+
+        @pl.when(pos > 0)
+        def _():
+            give(3, pos - 1)
 
         return c
-
-    lax.fori_loop(0, 32, first_loop, 0)
-    forward(2, 0)
-    lax.fori_loop(0, 32, second_loop, 0)
-    give(3, 31)
-    give(1, 31)
 
     q = lax.broadcasted_iota(jnp.int32, (64, 128), 0)
     hi_of = jnp.where(q < 32, 2 * q, 2 * q - 63)
@@ -239,88 +212,130 @@
         spread(i * 4)
         return c
 
-    def mix(k, group):
-        og, oc = order(group // 2), lax.rem(group, 2)
-
-        @pl.when(group < 6)
-        def _():
-            await_bytes(zone.at[k, og, pl.ds(oc * 4, 4)], rs2.at[k, og * 2 + oc])
-
-        @pl.when(group == 6)
-        def _():
-            await_bytes(zone.at[k, 0, 1:4], rs1.at[k, 6])
-
-        @pl.when(group == 7)
-        def _():
-            await_bytes(zone.at[k, 0, 4:8], rs1.at[k, 7])
-
-        cols = zone[k, og, pl.ds(oc * 4, 4)].reshape(512, probe_n)
-        slot = og + 4 * ((og + 3) // 4) + at[SECOND[k]] * (1 - (og + 3) // 4)
-        tags = [metas[k, slot, oc * 4 + u] for u in range(4)]
-        vals = [jnp.broadcast_to(t[0:1], (16, 128)).astype(bf16) for t in tags]
+    def mix(k, og, into):
+        turn = TURN[og]
+        await_bytes(zone.at[k, og, 1:4], rs1.at[k, 2 * turn])
+        await_bytes(zone.at[k, og, 4:8], rs1.at[k, 2 * turn + 1])
+        chan = lax.rem(at[SECOND[k]] + og, 4)
         zero = jnp.zeros((16, 128), bf16)
-        for m in range(4):
-            names = [jnp.broadcast_to(t[1:2] - float(m * 256), (16, 128)).astype(bf16) for t in tags]
-            mixer = jnp.concatenate(
-                [
-                    jnp.concatenate(
-                        [
-                            jnp.where(names[u] == steps_v[i * 16:(i + 1) * 16, :], vals[u], zero)
-                            for i in range(16)
-                        ],
-                        axis=0,
-                    )
-                    for u in range(4)
-                ],
-                axis=1,
-            )
-            part[k, m * 256:(m + 1) * 256, :] += jnp.dot(mixer, cols, preferred_element_type=f32)
-
-    def mix_loop(*kinds):
+
+        def block(m):
+            total = None
+            for oc in range(2):
+                tags = [metas[k, chan, oc * 4 + u] for u in range(4)]
+                vals = [jnp.broadcast_to(t[0:1], (16, 128)).astype(bf16) for t in tags]
+                base = (jnp.int32(m) * 256).astype(f32)
+                names = [jnp.broadcast_to(t[1:2] - base, (16, 128)).astype(bf16) for t in tags]
+                mixer = jnp.concatenate(
+                    [
+                        jnp.concatenate(
+                            [
+                                jnp.where(names[u] == steps_v[i * 16:(i + 1) * 16, :], vals[u], zero)
+                                for i in range(16)
+                            ],
+                            axis=0,
+                        )
+                        for u in range(4)
+                    ],
+                    axis=1,
+                )
+                cols = zone[k, og, oc * 4:oc * 4 + 4].reshape(512, probe_n)
+                got = jnp.dot(mixer, cols, preferred_element_type=f32)
+                total = got if total is None else total + got
+            into(m, total)
+
         def body(i, c):
-            for k in kinds:
-                mix(k, lax.rem(i + 6, 8))
+            for u in range(4):
+                block(i * 4 + u)
             return c
-        return body
+
+        lax.fori_loop(0, 4 // 4, body, 0)
+
+    def rows_at(m):
+        return pl.ds(pl.multiple_of(m * 256, 256), 256)
+
+    def step1(k):
+        def into(m, total):
+            total = total * dither[0:1, :]
+            out1[k, 0, rows_at(m), :] = total[:, :128].astype(bf16)
+            out1[k, 1, rows_at(m), :] = total[:, 128:].astype(bf16)
+
+        mix(k, 2, into)
+        ring1(k, 0).start()
+        ring1(k, 1).start()
+
+    def step2(k):
+        for half in (0, 1):
+            def into(m, total):
+                other = in1[k, half, rows_at(m), :].astype(f32)
+                left, right = total[:, :128], total[:, 128:]
+                if half == 0:
+                    left = left + other
+                else:
+                    right = right + other
+                out2[k, half, rows_at(m), :128] = (left * dither[0:1, :128]).astype(bf16)
+                out2[k, half, rows_at(m), 128:] = (right * dither[0:1, 128:]).astype(bf16)
+
+            await_bytes(in1.at[k, half], r1_sem.at[k, half])
+            mix(k, 1 + 2 * half, into)
+            ring2(k, half).start()
+
+    def own(k):
+        def into(m, total):
+            part[k, rows_at(m), :] = total
+
+        mix(k, 0, into)
+
+    def collect(k):
+        for half in (0, 1):
+            await_bytes(in2.at[k, half], r2_sem.at[k, half])
 
     def sum_up(k):
         for oh in (1, 3, 2):
-            block = lax.rem(at[THIRD[k]] + oh, 4)
-            rows = part[k, pl.ds(pl.multiple_of(block * 256, 256), 256), :]
+            block = rows_at(lax.rem(at[THIRD[k]] + oh, 4))
+            rows = part[k, block, :] + in2[k, 0, block, :].astype(f32) + in2[k, 1, block, :].astype(f32)
             parcel[k, oh - 1] = (rows * dither[0:1, :]).astype(bf16)
         for oh in (1, 3, 2):
             copy3(k, oh).start()
 
-    forward(2, 2)
-    for i in range(3):
-        forward(0, i)
-    forward(1, 0)
-    part[...] = jnp.zeros_like(part)
+    lax.fori_loop(0, 32, first_loop, 0)
+    for k in (2, 0, 1):
+        give(k, 31)
     for k in range(4):
-        await_bytes(metas.at[k, 5:8], m_sem.at[3, k])
+        await_bytes(metas.at[k, 0:4, 1:8], m_sem.at[1, k])
+    step1(2)
+    step1(1)
+    step1(0)
+    lax.fori_loop(0, 32, second_loop, 0)
+    give(3, 31)
+    step2(1)
+    step2(0)
+    step2(2)
+    step1(3)
+    own(1)
+    own(0)
     lax.fori_loop(0, 16, spread_loop, 0)
-    forward(3, 0)
-    forward(1, 1)
+    collect(1)
+    sum_up(1)
+    collect(0)
+    sum_up(0)
+    step2(3)
+    own(2)
+    own(3)
     lax.fori_loop(16, 32, spread_loop, 0)
-    lax.fori_loop(0, 4, mix_loop(2), 0)
-    forward(1, 2)
-    forward(3, 1)
-    lax.fori_loop(4, 8, mix_loop(2), 0)
+    collect(2)
     sum_up(2)
-    lax.fori_loop(0, 4, mix_loop(0), 0)
-    forward(3, 2)
-    lax.fori_loop(4, 8, mix_loop(0), 0)
-    sum_up(0)
-    lax.fori_loop(0, 8, mix_loop(1, 3), 0)
-    sum_up(1)
+    collect(3)
     sum_up(3)
 
     h_send[...] = jnp.zeros_like(h_send)
     ones = jnp.ones((8, 128), f32)
-    for k in (2, 0, 1, 3):
+    for k in (0, 1, 2, 3):
         await_bytes(final.at[k], fr.at[k])
         block = at[THIRD[k]]
-        whole = part[k, pl.ds(pl.multiple_of(block * 256, 256), 256), :]
+        whole = part[k, rows_at(block), :]
+        for half in (0, 1):
+            whole = whole + in2[k, half, rows_at(block), :].astype(f32)
         for i in range(3):
             whole = whole + final[k, i].astype(f32)
         whole = whole * whole
@@ -404,10 +419,10 @@
 
     for k in range(4):
         await_bytes(send.at[k, 0:28], sent.at[0, k])
-        await_bytes(zone.at[k, 1:4], sent.at[1, k])
+        await_bytes(in1.at[k], sent.at[1, k])
+        await_bytes(in2.at[k], sent.at[3, k])
         await_bytes(final.at[k], sent.at[2, k])
         await_bytes(metas.at[k, 0:4, 1:8], m_sem.at[0, k])
-        await_bytes(metas.at[k, 5:8], m_sem.at[2, k])
     await_bytes(h_in.at[1:8], h_sem.at[0])
     await_bytes(h_in2.at[1:16], h_sem.at[2])
 
@@ -443,13 +458,17 @@
             pltpu.VMEM((tile_r * tile_c, 2, 128), f32),
             pltpu.VMEM((3, 256, 128), f32),
             pltpu.VMEM((4, 32, nblk, probe_n), bf16),
-            pltpu.VMEM((4, 7, 8, nblk, probe_n), bf16),
+            pltpu.VMEM((4, 4, 8, nblk, probe_n), bf16),
             pltpu.VMEM((128, 2, 128), f32),
-            pltpu.VMEM((4, 8, 8, 2, 128), f32),
+            pltpu.VMEM((4, 4, 8, 2, 128), f32),
             pltpu.VMEM((nblk, foot), f32),
             pltpu.VMEM((nblk, foot), f32),
             pltpu.VMEM((nblk, 64, 128), f32),
             pltpu.VMEM((4, 1024, probe_n), f32),
+            pltpu.VMEM((4, 2, 1024, 128), bf16),
+            pltpu.VMEM((4, 2, 1024, 128), bf16),
+            pltpu.VMEM((4, 2, 1024, probe_n), bf16),
+            pltpu.VMEM((4, 2, 1024, probe_n), bf16),
             pltpu.VMEM((4, 3, 256, probe_n), bf16),
             pltpu.VMEM((4, 3, 256, probe_n), bf16),
             pltpu.VMEM((8, probe_n), f32),
@@ -459,7 +478,7 @@
             pltpu.VMEM((8, 128), f32),
             pltpu.VMEM((16, 8, 128), f32),
             pltpu.VMEM((128, 128), f32),
-            dma((4,)), dma(()), dma((3, 4)), dma((4, 8)), dma((4, 8)), dma((4, 4)), dma((4,)), dma((4,)),
+            dma((4,)), dma(()), dma((4, 4)), dma((4, 8)), dma((4, 2)), dma((4, 2)), dma((2, 4)), dma((4,)), dma((4,)),
         ],
         compiler_params=pltpu.CompilerParams(
             collective_id=0, has_side_effects=True, vmem_limit_bytes=60 * 2 ** 20

time: 103 us -> 97.2 us (0.944)
  Pallas kernels: 101 us -> 95.6 us
    pallas_call x1, Pallas kernels: 99.7 us -> 94.2 us  [local(): pl.pallas_call(kernel, out_shape=outs, in_specs=[anyw, vmem, anyw] + [vme...]
where the time goes in v6:
time: 97.2 us; the launch traced here: 96.9 us
  Pallas kernels  95.6 us (98%)
  between operations  1.29 us (1%)
    pallas_call x1, Pallas kernels, local(): pl.pallas_call(kernel, out_shape=outs, in_specs=[anyw, vmem, anyw] + [vme...  94.2 us

profile of v6, /device:TPU:1, one launch (start us, length us, event | category | flops | bytes accessed | tf_op | source)
XLA Modules:
  0.0 96.9 jit_solution(12037096004648546600)
XLA Ops:
  1.3 94.2 %exchange.1 = (f32[8]{0:T(128)}, f32[8,128]{1,0:T(8,128)}, f32[32,256]{1,0:T(8,128)}) custom-call(s32[16384]{0:T(1024)} %bitcast.9, s32[1,1]{1,0:T(1,128)} %bitcast.7.count_v, bf16[8192,256]{1,0:T(8,128)(2,1)} %bitcast.8, s32[128,128]{1,0:T(8,128)} %rows_v.1, bf16[128,128]{1,0:T(8,128)(2,1)} %coef_b.1, s32[1,128]{1,0:T(1,128)} %bitcast.12, ...), custom_call_target="tpu_custom_call" | custom-call | tf_op jit(solution)/shard_map/exchange/pallas_call | solution.py:450
  95.5 1.4 %finish.1 = (f32[8]{0:T(128)}, f32[8,128]{1,0:T(8,128)}, f32[32,256]{1,0:T(8,128)}) custom-call(f32[8]{0:T(128)} %get-tuple-element.9.sens, f32[8,128]{1,0:T(8,128)} %get-tuple-element.10.new, f32[32,256]{1,0:T(8,128)} %get-tuple-element.11.dens), custom_call_target="tpu_custom_call" | custom-call | tf_op jit(solution)/shard_map/finish/pallas_call | solution.py:491

commit v7 on v6

--- a/solution.py
+++ b/solution.py
@@ -7,9 +7,11 @@
 
 MESH = pl.DeviceIdType.MESH
 HIGHEST = lax.Precision.HIGHEST
-FIRST = (0, 1, 2, 0)
-SECOND = (1, 2, 0, 1)
-THIRD = (2, 0, 1, 2)
+FIRST = (0, 1, 2, 0, 2)
+SECOND = (1, 2, 0, 1, 1)
+THIRD = (2, 0, 1, 2, 0)
+BASE = (0, 16, 32, 48, 48)
+KINDS = (0, 1, 2, 3, 4)
 TURN = {2: 0, 1: 1, 3: 2, 0: 3}
 
 
@@ -36,8 +38,9 @@
 def kernel(
     rows_h, count_v, probes_h, rows_v, coef_b, ids_r, owner_v, weights_v,
     sens_o, new_o, dens_o,
-    rows_s, probes, tile, stage, send, zone, meta, metas, coef_v, ids_v, dens, part,
-    out1, in1, out2, in2, parcel, final, dither, steps_v,
+    rows_s, probes, tile, stage, meta, metas, coef_v, ids_v, dens, dither, steps_v,
+    send_w, zone_w, part_w, out1_w, in1_w, out2_w, in2_w, parcel_w, final_w,
+    send_n, zone_n, part_n, out1_n, in1_n, out2_n, in2_n, parcel_n, final_n,
     h_send, h_in, h_mid, h_in2, wide,
     in_sem, row_sem, sent, rs1, r1_sem, r2_sem, m_sem, fr, h_sem,
 ):
@@ -48,6 +51,15 @@
     me = gx * 8 + gy
     at, core = place()
     bf16, f32 = jnp.bfloat16, jnp.float32
+
+    def by_kind(wide_ref, narrow_ref):
+        return [wide_ref.at[i] for i in range(3)] + [narrow_ref.at[i] for i in range(2)]
+
+    send, zone, part = by_kind(send_w, send_n), by_kind(zone_w, zone_n), by_kind(part_w, part_n)
+    out1, in1 = by_kind(out1_w, out1_n), by_kind(in1_w, in1_n)
+    out2, in2 = by_kind(out2_w, out2_n), by_kind(in2_w, in2_n)
+    parcel, final = by_kind(parcel_w, parcel_n), by_kind(final_w, final_n)
+    lanes = [slice(0, 256)] * 3 + [slice(0, 128), slice(128, 256)]
 
     def load(i):
         part_of = pl.ds(i * chunk, chunk)
@@ -101,7 +113,7 @@
         ).astype(f32).astype(bf16)
 
     def meta1(k, of, oc):
-        first = lax.rem(core + oc, 2) * 64 + k * 16 + lax.rem(at[FIRST[k]] + of, 4) * 4
+        first = lax.rem(core + oc, 2) * 64 + BASE[k] + lax.rem(at[FIRST[k]] + of, 4) * 4
         src = oc * 4 + of
         return pltpu.make_async_remote_copy(
             src_ref=meta.at[pl.ds(first, 4)], dst_ref=metas.at[k, pl.ds(0, 4), src],
@@ -112,21 +124,21 @@
     def copy1(k, pos):
         og, of, oc = decode(pos)
         return pltpu.make_async_remote_copy(
-            src_ref=send.at[k, pos], dst_ref=zone.at[k, og, oc * 4 + of],
+            src_ref=send[k].at[pos], dst_ref=zone[k].at[og, oc * 4 + of],
             send_sem=sent.at[0, k], recv_sem=rs1.at[k, pos // 4],
             device_id=peer(FIRST[k], of, oc), device_id_type=MESH,
         )
 
     def ring1(k, half):
         return pltpu.make_async_remote_copy(
-            src_ref=out1.at[k, half], dst_ref=in1.at[k, half],
+            src_ref=out1[k].at[half], dst_ref=in1[k].at[half],
             send_sem=sent.at[1, k], recv_sem=r1_sem.at[k, half],
             device_id=peer(SECOND[k], 1 + 2 * half, 0), device_id_type=MESH,
         )
 
     def ring2(k, half):
         return pltpu.make_async_remote_copy(
-            src_ref=out2.at[k, half], dst_ref=in2.at[k, half],
+            src_ref=out2[k].at[half], dst_ref=in2[k].at[half],
             send_sem=sent.at[3, k], recv_sem=r2_sem.at[k, half],
             device_id=peer(SECOND[k], 1 + 2 * half, 0), device_id_type=MESH,
         )
@@ -136,25 +148,37 @@
 
     def copy3(k, oh):
         return pltpu.make_async_remote_copy(
-            src_ref=parcel.at[k, oh - 1], dst_ref=final.at[k, oh - 1],
+            src_ref=parcel[k].at[oh - 1], dst_ref=final[k].at[oh - 1],
             send_sem=sent.at[2, k], recv_sem=fr.at[k],
             device_id=peer(THIRD[k], oh, 0), device_id_type=MESH,
         )
 
     others = [(of, oc) for oc in (0, 1) for of in (1, 3, 2, 0) if (of, oc) != (0, 0)]
-    for k in range(4):
-        metas[k, 0:4, 0] = meta[pl.ds(core * 64 + k * 16 + at[FIRST[k]] * 4, 4)]
+    for k in KINDS:
+        metas[k, 0:4, 0] = meta[pl.ds(core * 64 + BASE[k] + at[FIRST[k]] * 4, 4)]
 
     def gather(k, pos, buf):
         og, of, oc = decode(pos)
         chan = (
-            lax.rem(core + oc, 2) * 64 + k * 16
+            lax.rem(core + oc, 2) * 64 + BASE[k]
             + lax.rem(at[FIRST[k]] + of, 4) * 4 + lax.rem(at[SECOND[k]] + og, 4)
         )
         for i in range(128):
             stage[buf, 2 * i:2 * i + 2, :] = tile[rows_s[chan + i * 128]]
-        send[k, pos, :, :128] = stage[buf, pl.ds(0, 128, 2), :].astype(bf16)
-        send[k, pos, :, 128:] = stage[buf, pl.ds(1, 128, 2), :].astype(bf16)
+        left = stage[buf, pl.ds(0, 128, 2), :].astype(bf16)
+        right = stage[buf, pl.ds(1, 128, 2), :].astype(bf16)
+        if k < 3:
+            send[k][pos, :, :128] = left
+            send[k][pos, :, 128:] = right
+        else:
+            send[3][pos] = left
+            send[4][twin(pos)] = right
+
+    def twin(pos):
+        _, of, _ = decode(pos)
+        of = lax.rem(of + at[0] - at[2] + 4, 4)
+        a, b = lax.rem(of, 2), of // 2
+        return pos // 4 * 4 + 3 - 3 * a - b + 2 * a * b
 
     def give(k, pos):
         mine = lax.rem(pos, 8) == 3
@@ -162,7 +186,7 @@
         @pl.when(mine)
         def _():
             og, _, _ = decode(pos)
-            zone[k, og, 0] = send[k, pos]
+            zone[k][og, 0] = send[k][pos]
 
         @pl.when(jnp.logical_not(mine))
         def _():
@@ -176,7 +200,7 @@
                 def _():
                     pl.semaphore_wait(barrier, 28)
                     for of, oc in others:
-                        for j in range(4):
+                        for j in KINDS:
                             meta1(j, of, oc).start()
 
             @pl.when(pos > 0)
@@ -191,6 +215,7 @@
         @pl.when(pos > 0)
         def _():
             give(3, pos - 1)
+            give(4, twin(pos - 1))
 
         return c
 
@@ -214,17 +239,17 @@
 
     def mix(k, og, into):
         turn = TURN[og]
-        await_bytes(zone.at[k, og, 1:4], rs1.at[k, 2 * turn])
-        await_bytes(zone.at[k, og, 4:8], rs1.at[k, 2 * turn + 1])
+        await_bytes(zone[k].at[og, 1:4], rs1.at[k, 2 * turn])
+        await_bytes(zone[k].at[og, 4:8], rs1.at[k, 2 * turn + 1])
         chan = lax.rem(at[SECOND[k]] + og, 4)
         zero = jnp.zeros((16, 128), bf16)
 
-        def block(m):
+        for m in range(4):
             total = None
             for oc in range(2):
                 tags = [metas[k, chan, oc * 4 + u] for u in range(4)]
                 vals = [jnp.broadcast_to(t[0:1], (16, 128)).astype(bf16) for t in tags]
-                base = (jnp.int32(m) * 256).astype(f32)
+                base = float(m * 256)
                 names = [jnp.broadcast_to(t[1:2] - base, (16, 128)).astype(bf16) for t in tags]
                 mixer = jnp.concatenate(
                     [
@@ -239,26 +264,19 @@
                     ],
                     axis=1,
                 )
-                cols = zone[k, og, oc * 4:oc * 4 + 4].reshape(512, probe_n)
+                cols = zone[k][og, oc * 4:oc * 4 + 4].reshape(512, 256 if k < 3 else 128)
                 got = jnp.dot(mixer, cols, preferred_element_type=f32)
                 total = got if total is None else total + got
             into(m, total)
 
-        def body(i, c):
-            for u in range(4):
-                block(i * 4 + u)
-            return c
-
-        lax.fori_loop(0, 4 // 4, body, 0)
-
     def rows_at(m):
         return pl.ds(pl.multiple_of(m * 256, 256), 256)
 
     def step1(k):
         def into(m, total):
-            total = total * dither[0:1, :]
-            out1[k, 0, rows_at(m), :] = total[:, :128].astype(bf16)
-            out1[k, 1, rows_at(m), :] = total[:, 128:].astype(bf16)
+            out1[k][m // 2, m % 2 * 256:m % 2 * 256 + 256, :] = (
+                total * dither[0:1, lanes[k]]
+            ).astype(bf16)
 
         mix(k, 2, into)
         ring1(k, 0).start()
@@ -267,80 +285,86 @@
     def step2(k):
         for half in (0, 1):
             def into(m, total):
-                other = in1[k, half, rows_at(m), :].astype(f32)
-                left, right = total[:, :128], total[:, 128:]
-                if half == 0:
-                    left = left + other
-                else:
-                    right = right + other
-                out2[k, half, rows_at(m), :128] = (left * dither[0:1, :128]).astype(bf16)
-                out2[k, half, rows_at(m), 128:] = (right * dither[0:1, 128:]).astype(bf16)
-
-            await_bytes(in1.at[k, half], r1_sem.at[k, half])
+                if m // 2 == half:
+                    total = total + in1[k][half, m % 2 * 256:m % 2 * 256 + 256, :].astype(f32)
+                out2[k][half, m * 256:m * 256 + 256, :] = (total * dither[0:1, lanes[k]]).astype(bf16)
+
+            await_bytes(in1[k].at[half], r1_sem.at[k, half])
             mix(k, 1 + 2 * half, into)
             ring2(k, half).start()
 
     def own(k):
         def into(m, total):
-            part[k, rows_at(m), :] = total
+            part[k][m * 256:m * 256 + 256, :] = total
 
         mix(k, 0, into)
 
     def collect(k):
         for half in (0, 1):
-            await_bytes(in2.at[k, half], r2_sem.at[k, half])
+            await_bytes(in2[k].at[half], r2_sem.at[k, half])
+
+    def summed(k, block):
+        rows = part[k][rows_at(block), :]
+        for half in (0, 1):
+            rows = rows + in2[k][half, rows_at(block), :].astype(f32)
+        return rows
 
     def sum_up(k):
         for oh in (1, 3, 2):
-            block = rows_at(lax.rem(at[THIRD[k]] + oh, 4))
-            rows = part[k, block, :] + in2[k, 0, block, :].astype(f32) + in2[k, 1, block, :].astype(f32)
-            parcel[k, oh - 1] = (rows * dither[0:1, :]).astype(bf16)
+            rows = summed(k, lax.rem(at[THIRD[k]] + oh, 4))
+            parcel[k][oh - 1] = (rows * dither[0:1, lanes[k]]).astype(bf16)
         for oh in (1, 3, 2):
             copy3(k, oh).start()
 
     lax.fori_loop(0, 32, first_loop, 0)
     for k in (2, 0, 1):
         give(k, 31)
-    for k in range(4):
+    for k in KINDS:
         await_bytes(metas.at[k, 0:4, 1:8], m_sem.at[1, k])
     step1(2)
     step1(1)
     step1(0)
     lax.fori_loop(0, 32, second_loop, 0)
     give(3, 31)
+    give(4, twin(31))
+    step2(0)
     step2(1)
-    step2(0)
     step2(2)
     step1(3)
+    step1(4)
     own(1)
     own(0)
     lax.fori_loop(0, 16, spread_loop, 0)
-    collect(1)
-    sum_up(1)
+    own(2)
+    lax.fori_loop(16, 32, spread_loop, 0)
     collect(0)
     sum_up(0)
     step2(3)
-    own(2)
+    step2(4)
     own(3)
-    lax.fori_loop(16, 32, spread_loop, 0)
+    own(4)
+    collect(1)
+    sum_up(1)
     collect(2)
     sum_up(2)
     collect(3)
     sum_up(3)
+    collect(4)
+    sum_up(4)
 
     h_send[...] = jnp.zeros_like(h_send)
     ones = jnp.ones((8, 128), f32)
-    for k in (0, 1, 2, 3):
-        await_bytes(final.at[k], fr.at[k])
+    for k in KINDS:
+        await_bytes(final[k], fr.at[k])
         block = at[THIRD[k]]
-        whole = part[k, rows_at(block), :]
-        for half in (0, 1):
-            whole = whole + in2[k, half, rows_at(block), :].astype(f32)
+        whole = summed(k, block)
         for i in range(3):
-            whole = whole + final[k, i].astype(f32)
+            whole = whole + final[k][i].astype(f32)
         whole = whole * whole
+        if k < 3:
+            whole = whole[:, :128] + whole[:, 128:]
         sums = lax.dot_general(
-            ones, whole[:, :128] + whole[:, 128:], (((1,), (1,)), ((), ())),
+            ones, whole, (((1,), (1,)), ((), ())),
             preferred_element_type=f32, precision=HIGHEST,
         ) * (1.0 / (foot * probe_n))
         for i in range(2):
@@ -417,11 +441,11 @@
     dens_o[:, :128] = out[:32]
     dens_o[:, 128:] = out[32:]
 
-    for k in range(4):
-        await_bytes(send.at[k, 0:28], sent.at[0, k])
-        await_bytes(in1.at[k], sent.at[1, k])
-        await_bytes(in2.at[k], sent.at[3, k])
-        await_bytes(final.at[k], sent.at[2, k])
+    for k in KINDS:
+        await_bytes(send[k].at[0:28], sent.at[0, k])
+        await_bytes(in1[k], sent.at[1, k])
+        await_bytes(in2[k], sent.at[3, k])
+        await_bytes(final[k], sent.at[2, k])
         await_bytes(metas.at[k, 0:4, 1:8], m_sem.at[0, k])
     await_bytes(h_in.at[1:8], h_sem.at[0])
     await_bytes(h_in2.at[1:16], h_sem.at[2])
@@ -457,28 +481,27 @@
             pltpu.VMEM((tile_r * tile_c, probe_n), bf16),
             pltpu.VMEM((tile_r * tile_c, 2, 128), f32),
             pltpu.VMEM((3, 256, 128), f32),
-            pltpu.VMEM((4, 32, nblk, probe_n), bf16),
-            pltpu.VMEM((4, 4, 8, nblk, probe_n), bf16),
             pltpu.VMEM((128, 2, 128), f32),
-            pltpu.VMEM((4, 4, 8, 2, 128), f32),
+            pltpu.VMEM((5, 4, 8, 2, 128), f32),
             pltpu.VMEM((nblk, foot), f32),
             pltpu.VMEM((nblk, foot), f32),
             pltpu.VMEM((nblk, 64, 128), f32),
-            pltpu.VMEM((4, 1024, probe_n), f32),
-            pltpu.VMEM((4, 2, 1024, 128), bf16),
-            pltpu.VMEM((4, 2, 1024, 128), bf16),
-            pltpu.VMEM((4, 2, 1024, probe_n), bf16),
-            pltpu.VMEM((4, 2, 1024, probe_n), bf16),
-            pltpu.VMEM((4, 3, 256, probe_n), bf16),
-            pltpu.VMEM((4, 3, 256, probe_n), bf16),
             pltpu.VMEM((8, probe_n), f32),
             pltpu.VMEM((256, 128), bf16),
+            *[
+                pltpu.VMEM((kinds, *dims, width), kind)
+                for kinds, width in ((3, probe_n), (2, probe_n // 2))
+                for dims, kind in (
+                    ((32, nblk), bf16), ((4, 8, nblk), bf16), ((1024,), f32), ((2, 512), bf16), ((2, 512), bf16),
+                    ((2, 1024), bf16), ((2, 1024), bf16), ((3, 256), bf16), ((3, 256), bf16),
+                )
+            ],
             pltpu.VMEM((8, 128), f32),
             pltpu.VMEM((8, 8, 128), f32),
             pltpu.VMEM((8, 128), f32),
             pltpu.VMEM((16, 8, 128), f32),
             pltpu.VMEM((128, 128), f32),
-            dma((4,)), dma(()), dma((4, 4)), dma((4, 8)), dma((4, 2)), dma((4, 2)), dma((2, 4)), dma((4,)), dma((4,)),
+            dma((4,)), dma(()), dma((4, 5)), dma((5, 8)), dma((5, 2)), dma((5, 2)), dma((2, 5)), dma((5,)), dma((4,)),
         ],
         compiler_params=pltpu.CompilerParams(
             collective_id=0, has_side_effects=True, vmem_limit_bytes=60 * 2 ** 20

time: 97.2 us -> 92.7 us (0.954)
  Pallas kernels: 95.6 us -> 91 us
    pallas_call x1, Pallas kernels: 94.2 us -> 89.6 us  [local(): pl.pallas_call(kernel, out_shape=outs, in_specs=[anyw, vmem, anyw] + [vme...]
where the time goes in v7:
time: 92.7 us; the launch traced here: 92.5 us
  Pallas kernels  91 us (98%)
  between operations  1.45 us (2%)
    pallas_call x1, Pallas kernels, local(): pl.pallas_call(kernel, out_shape=outs, in_specs=[anyw, vmem, anyw] + [vme...  89.6 us

profile of v7, /device:TPU:1, one launch (start us, length us, event | category | flops | bytes accessed | tf_op | source)
XLA Modules:
  0.0 92.5 jit_solution(548624291004387367)
XLA Ops:
  1.3 89.6 %exchange.1 = (f32[8]{0:T(128)}, f32[8,128]{1,0:T(8,128)}, f32[32,256]{1,0:T(8,128)}) custom-call(s32[16384]{0:T(1024)} %bitcast.9, s32[1,1]{1,0:T(1,128)} %bitcast.7.count_v, bf16[8192,256]{1,0:T(8,128)(2,1)} %bitcast.8, s32[128,128]{1,0:T(8,128)} %rows_v.1, bf16[128,128]{1,0:T(8,128)(2,1)} %coef_b.1, s32[1,128]{1,0:T(1,128)} %bitcast.12, ...), custom_call_target="tpu_custom_call" | custom-call | tf_op jit(solution)/shard_map/exchange/pallas_call | solution.py:474
  90.9 1.4 %finish.1 = (f32[8]{0:T(128)}, f32[8,128]{1,0:T(8,128)}, f32[32,256]{1,0:T(8,128)}) custom-call(f32[8]{0:T(128)} %get-tuple-element.9.sens, f32[8,128]{1,0:T(8,128)} %get-tuple-element.10.new, f32[32,256]{1,0:T(8,128)} %get-tuple-element.11.dens), custom_call_target="tpu_custom_call" | custom-call | tf_op jit(solution)/shard_map/finish/pallas_call | solution.py:514

commit v8 on v7

--- a/solution.py
+++ b/solution.py
@@ -193,7 +193,7 @@
             copy1(k, pos).start()
 
     def first_loop(pos, c):
-        for buf, k in enumerate((2, 0, 1)):
+        for buf, k in enumerate((1, 2, 0)):
             gather(k, pos, buf)
             if buf == 0:
                 @pl.when(pos == 1)
@@ -317,13 +317,13 @@
             copy3(k, oh).start()
 
     lax.fori_loop(0, 32, first_loop, 0)
-    for k in (2, 0, 1):
+    for k in (1, 2, 0):
         give(k, 31)
     for k in KINDS:
         await_bytes(metas.at[k, 0:4, 1:8], m_sem.at[1, k])
+    step1(0)
+    step1(1)
     step1(2)
-    step1(1)
-    step1(0)
     lax.fori_loop(0, 32, second_loop, 0)
     give(3, 31)
     give(4, twin(31))
@@ -386,7 +386,7 @@
             device_id=(to, gy), device_id_type=MESH,
         )
 
-    for k in range(1, 8):
+    for k in (5, 4, 3, 7, 2, 6, 1):
         first_copy(k).start()
     h_in[gy] = h_send[...]
     mine = owner_v[...] == me
@@ -410,7 +410,7 @@
     for k in range(1, 8):
         total = total + h_in[k]
     h_mid[...] = total
-    for k in range(1, 16):
+    for k in (10, 6, 14, 9, 11, 2, 8, 5, 15, 7, 13, 1, 3, 4, 12):
         second_copy(k).start()
     h_in2[gx] = total
     await_bytes(h_in2.at[1:16], h_sem.at[3])

time: 92.7 us -> 92.3 us (level)
  no operation moved by 1% of the time
where the time goes in v8:
time: 92.3 us; the launch traced here: 92 us
  Pallas kernels  90.6 us (98%)
  between operations  1.45 us (2%)
    pallas_call x1, Pallas kernels, local(): pl.pallas_call(kernel, out_shape=outs, in_specs=[anyw, vmem, anyw] + [vme...  89.2 us

profile of v8, /device:TPU:1, one launch (start us, length us, event | category | flops | bytes accessed | tf_op | source)
XLA Modules:
  0.0 92.0 jit_solution(14887519799999711134)
XLA Ops:
  1.3 89.2 %exchange.1 = (f32[8]{0:T(128)}, f32[8,128]{1,0:T(8,128)}, f32[32,256]{1,0:T(8,128)}) custom-call(s32[16384]{0:T(1024)} %bitcast.9, s32[1,1]{1,0:T(1,128)} %bitcast.7.count_v, bf16[8192,256]{1,0:T(8,128)(2,1)} %bitcast.8, s32[128,128]{1,0:T(8,128)} %rows_v.1, bf16[128,128]{1,0:T(8,128)(2,1)} %coef_b.1, s32[1,128]{1,0:T(1,128)} %bitcast.12, ...), custom_call_target="tpu_custom_call" | custom-call | tf_op jit(solution)/shard_map/exchange/pallas_call | solution.py:474
  90.5 1.4 %finish.1 = (f32[8]{0:T(128)}, f32[8,128]{1,0:T(8,128)}, f32[32,256]{1,0:T(8,128)}) custom-call(f32[8]{0:T(128)} %get-tuple-element.9.sens, f32[8,128]{1,0:T(8,128)} %get-tuple-element.10.new, f32[32,256]{1,0:T(8,128)} %get-tuple-element.11.dens), custom_call_target="tpu_custom_call" | custom-call | tf_op jit(solution)/shard_map/finish/pallas_call | solution.py:514
